TPU v7x, 32 devices: a whole 2x2x4 slice. The times are simulated.
32 devices in a mesh: layer: 2 (over x), tp: 4 (over z), fsdp: 4 (over y, core).
Axes of the slice: x: 2, y: 2, z: 4, core: 2. Of those that a mesh axis runs over, the one named last changes fastest.
Arguments:
- wq_weight: float32 [4096, 2048], P(('layer', 'fsdp'), 'tp'), parts along dimension 0
- wq_moment: float32 [4096, 2048], P(('layer', 'fsdp'), 'tp'), parts along dimension 0
- wq_grad: bfloat16 [4096, 2048], P(('layer', 'fsdp'), 'tp'), parts along dimension 0
- wq_factor: float32 [4096, 128], P(('layer', 'tp')), parts along dimension 0
- wk_weight: float32 [4096, 2048], P(('layer', 'fsdp'), 'tp'), parts along dimension 0
- wk_moment: float32 [4096, 2048], P(('layer', 'fsdp'), 'tp'), parts along dimension 0
- wk_grad: bfloat16 [4096, 2048], P(('layer', 'fsdp'), 'tp'), parts along dimension 0
- wk_factor: float32 [4096, 128], P(('layer', 'tp')), parts along dimension 0
- wv_weight: float32 [4096, 2048], P(('layer', 'fsdp'), 'tp'), parts along dimension 0
- wv_moment: float32 [4096, 2048], P(('layer', 'fsdp'), 'tp'), parts along dimension 0
- wv_grad: bfloat16 [4096, 2048], P(('layer', 'fsdp'), 'tp'), parts along dimension 0
- wv_factor: float32 [4096, 128], P(('layer', 'tp')), parts along dimension 0
- wo_weight: float32 [4096, 2048], P(('layer', 'fsdp'), 'tp'), parts along dimension 0
- wo_moment: float32 [4096, 2048], P(('layer', 'fsdp'), 'tp'), parts along dimension 0
- wo_grad: bfloat16 [4096, 2048], P(('layer', 'fsdp'), 'tp'), parts along dimension 0
- wo_factor: float32 [4096, 128], P(('layer', 'tp')), parts along dimension 0
- gate_weight: float32 [6, 2048, 1408], P('layer', 'fsdp', 'tp'), parts along dimension 0
- gate_moment: float32 [6, 2048, 1408], P('layer', 'fsdp', 'tp'), parts along dimension 0
- gate_grad: bfloat16 [6, 2048, 1408], P('layer', 'fsdp', 'tp'), parts along dimension 0
- gate_factor: float32 [6, 1408, 88], P('layer', 'tp'), parts along dimension 0
- up_weight: float32 [6, 2048, 1408], P('layer', 'fsdp', 'tp'), parts along dimension 0
- up_moment: float32 [6, 2048, 1408], P('layer', 'fsdp', 'tp'), parts along dimension 0
- up_grad: bfloat16 [6, 2048, 1408], P('layer', 'fsdp', 'tp'), parts along dimension 0
- up_factor: float32 [6, 1408, 88], P('layer', 'tp'), parts along dimension 0
- down_weight: float32 [6, 1408, 2048], P('layer', 'fsdp', 'tp'), parts along dimension 0
- down_moment: float32 [6, 1408, 2048], P('layer', 'fsdp', 'tp'), parts along dimension 0
- down_grad: bfloat16 [6, 1408, 2048], P('layer', 'fsdp', 'tp'), parts along dimension 0
- down_factor: float32 [6, 1408, 88], P('layer', 'fsdp'), parts along dimension 0
Outputs:
- output 1: float32 [4096, 2048], P(('layer', 'fsdp'), 'tp'), parts along dimension 0
- output 2: float32 [4096, 2048], P(('layer', 'fsdp'), 'tp'), parts along dimension 0
- output 3: float32 [4096, 128], P(('layer', 'tp')), parts along dimension 0
- output 4: float32 [4096, 2048], P(('layer', 'fsdp'), 'tp'), parts along dimension 0
- output 5: float32 [4096, 2048], P(('layer', 'fsdp'), 'tp'), parts along dimension 0
- output 6: float32 [4096, 128], P(('layer', 'tp')), parts along dimension 0
- output 7: float32 [4096, 2048], P(('layer', 'fsdp'), 'tp'), parts along dimension 0
- output 8: float32 [4096, 2048], P(('layer', 'fsdp'), 'tp'), parts along dimension 0
- output 9: float32 [4096, 128], P(('layer', 'tp')), parts along dimension 0
- output 10: float32 [4096, 2048], P(('layer', 'fsdp'), 'tp'), parts along dimension 0
- output 11: float32 [4096, 2048], P(('layer', 'fsdp'), 'tp'), parts along dimension 0
- output 12: float32 [4096, 128], P(('layer', 'tp')), parts along dimension 0
- output 13: float32 [6, 2048, 1408], P('layer', 'fsdp', 'tp'), parts along dimension 0
- output 14: float32 [6, 2048, 1408], P('layer', 'fsdp', 'tp'), parts along dimension 0
- output 15: float32 [6, 1408, 88], P('layer', 'tp'), parts along dimension 0
- output 16: float32 [6, 2048, 1408], P('layer', 'fsdp', 'tp'), parts along dimension 0
- output 17: float32 [6, 2048, 1408], P('layer', 'fsdp', 'tp'), parts along dimension 0
- output 18: float32 [6, 1408, 88], P('layer', 'tp'), parts along dimension 0
- output 19: float32 [6, 1408, 2048], P('layer', 'fsdp', 'tp'), parts along dimension 0
- output 20: float32 [6, 1408, 2048], P('layer', 'fsdp', 'tp'), parts along dimension 0
- output 21: float32 [6, 1408, 88], P('layer', 'fsdp'), parts along dimension 0
There are 2 independent parts. A program takes and returns all parts, laid end to end along the dimension named above; each array names one.
All inputs are finite; a program needn't handle non-finite values.
Results may differ from a plain program's by a relative error of at most 0.001.
Values are sent between devices in bfloat16 or wider.
A program may use at most 1 GiB of HBM per device.

v0:
```python
import math
import jax
import jax.numpy as jnp
from jax import lax
from jax.sharding import PartitionSpec as P

MOMENTUM = 0.9
LEARN_RATE = 0.3
FULL_PREC = lax.Precision.HIGHEST
KEEP_FORMS = ('bmn,bnr->bmr', 'bmn,bmr->bnr', 'bmr,bnr->bmn')
FLIP_FORMS = ('bnm,bnr->bmr', 'bnm,bmr->bnr', 'bmr,bnr->bnm')


def mat_mul(form, left_op, right_op):
    return jnp.einsum(form, left_op, right_op, preferred_element_type=jnp.float32, precision=FULL_PREC)


def dion_local(weight, moment, gradient, factor, forms, long_axis, short_axis, long_size, short_size):
    mom_grad = moment + gradient.astype(jnp.float32)
    p_tilde = lax.psum(mat_mul(forms[0], mom_grad, factor), short_axis)
    gram_mat = lax.psum(mat_mul('bmr,bms->brs', p_tilde, p_tilde), long_axis)
    chol_low = jnp.linalg.cholesky(gram_mat)
    p_orth = lax.linalg.triangular_solve(chol_low, p_tilde, left_side=False, lower=True, transpose_a=True)
    r_new = lax.psum(mat_mul(forms[1], mom_grad, p_orth), long_axis)
    moment_new = mom_grad - (1.0 - MOMENTUM) * mat_mul(forms[2], p_orth, r_new)
    col_sq = lax.psum(jnp.sum(r_new * r_new, axis=1, keepdims=True), short_axis)
    factor_new = r_new / jnp.sqrt(col_sq)
    step_scale = LEARN_RATE * math.sqrt(p_tilde.shape[1] * long_size / (factor.shape[1] * short_size))
    weight_new = weight - step_scale * mat_mul(forms[2], p_orth, factor_new)
    return weight_new, moment_new, factor_new


def solution(mesh):
    fsdp_size = mesh.shape['fsdp']
    tp_size = mesh.shape['tp']
    dense_w = P(('layer', 'fsdp'), 'tp')
    dense_f = P(('layer', 'tp'), None)
    stack_w = P('layer', 'fsdp', 'tp')
    stack_f = P('layer', 'tp', None)
    down_f = P('layer', 'fsdp', None)
    in_specs = (dense_w, dense_w, dense_w, dense_f) * 4 + (stack_w, stack_w, stack_w, stack_f) * 2 + (stack_w, stack_w, stack_w, down_f)
    out_specs = (dense_w, dense_w, dense_f) * 4 + (stack_w, stack_w, stack_f) * 2 + (stack_w, stack_w, down_f)

    def local_step(*blocks):
        results = []
        for mat_idx in range(4):
            group_in = [local_arr[None] for local_arr in blocks[4 * mat_idx:4 * mat_idx + 4]]
            updated = dion_local(group_in[0], group_in[1], group_in[2], group_in[3], KEEP_FORMS, 'fsdp', 'tp', fsdp_size, tp_size)
            results.extend([item_out[0] for item_out in updated])
        for mat_idx in (4, 5):
            group_in = blocks[4 * mat_idx:4 * mat_idx + 4]
            results.extend(dion_local(group_in[0], group_in[1], group_in[2], group_in[3], KEEP_FORMS, 'fsdp', 'tp', fsdp_size, tp_size))
        group_in = blocks[24:28]
        results.extend(dion_local(group_in[0], group_in[1], group_in[2], group_in[3], FLIP_FORMS, 'tp', 'fsdp', tp_size, fsdp_size))
        return tuple(results)

    return jax.shard_map(local_step, mesh=mesh, in_specs=in_specs, out_specs=out_specs, check_vma=False)
```

profile of v0, /device:TPU:0, one launch (start us, length us, event | category | flops | bytes accessed | tf_op | source)
XLA Modules:
  0.0 579.5 jit_solution(1481000921870836144)
XLA Ops:
  8.2 4.6 fusion.11
  12.9 2.6 fusion.9
  15.6 1.7 convolution_bitcast_fusion.11
  17.3 1.7 convolution_bitcast_fusion.14
  19.0 1.7 convolution_bitcast_fusion.5
  20.7 1.7 convolution_bitcast_fusion.8
  22.7 3.6 fusion.13
  26.3 86.2 %all-reduce.18.cloned.1.call-done = (f32[1,512,128]{2,1,0:T(8,128)}, f32[1,512,128]{2,1,0:T(8,128)}, f32[1,512,128]{2,1,0:T(8,128)}, f32[1,512,128]{2,1,0:T(8,12...) async-done(((f32[1,512,128]{2,1,0:T(8,128)}, f32[1,512,128]{2,1,0:T(8,128)}, f32[1,512,128]{2,1,0:T(8,128)}, f32[1,512,128]{2,1,0:T(8,128)}, f32[3,512,88]{1,2,0:T(8,128)}, ...) | async-done | bytes 2129936 | tf_op jit(solution)/shard_map/psum | solution.py:20
  112.5 2.6 fusion.44
  115.1 2.5 fusion.45
  122.6 36.4 %all-reduce.16.cloned.1.call-done = (f32[1,128,128]{1,2,0:T(8,128)}, f32[1,128,128]{1,2,0:T(8,128)}, f32[1,128,128]{1,2,0:T(8,128)}, f32[1,128,128]{1,2,0:T(8,12...) async-done(((f32[1,128,128]{1,2,0:T(8,128)}, f32[1,128,128]{1,2,0:T(8,128)}, f32[1,128,128]{1,2,0:T(8,128)}, f32[1,128,128]{1,2,0:T(8,128)}, ...) | async-done | bytes 988688 | tf_op jit(solution)/shard_map/psum | solution.py:21
  159.1 1.7 copy.75
  160.8 1.7 copy.78
  162.5 2.5 fusion.46
  168.0 12.5 %custom-call.28 = f32[1,128,128]{2,1,0:T(8,128)S(1)} custom-call(f32[1,128,128]{2,1,0:T(8,128)} %get-tuple-element.58), custom_call_target="Cholesky" | custom-call | tf_op jit(solution)/shard_map/jit(cholesky)/cholesky | solution.py:22
  181.9 10.4 %custom-call.29 = f32[1,1,128,128]{2,3,1,0:T(8,128)} custom-call(f32[1,1,128,128]{3,2,1,0:T(8,128)S(1)} %fusion.35), custom_call_target="InvertDiagBlocksLowerTriangular" | custom-call | tf_op jit(solution)/shard_map/triangular_solve/custom-call.2 | solution.py:23
  193.8 3.9 convolution_bitcast_fusion.3
  197.6 13.2 %custom-call.26 = f32[1,128,128]{2,1,0:T(8,128)} custom-call(f32[1,128,128]{2,1,0:T(8,128)} %get-tuple-element.59), custom_call_target="Cholesky" | custom-call | tf_op jit(solution)/shard_map/jit(cholesky)/cholesky | solution.py:22
  212.5 2.1 fusion.34
  214.6 11.3 %custom-call.27 = f32[1,1,128,128]{2,3,1,0:T(8,128)} custom-call(f32[1,1,128,128]{3,2,1,0:T(8,128)} %fusion.34), custom_call_target="InvertDiagBlocksLowerTriangular" | custom-call | tf_op jit(solution)/shard_map/triangular_solve/custom-call.2 | solution.py:23
  228.0 3.9 convolution_bitcast_fusion.6
  231.9 1.6 copy.67
  235.0 1.6 fusion.41
  236.6 13.2 %custom-call.24 = f32[1,128,128]{2,1,0:T(8,128)} custom-call(f32[1,128,128]{2,1,0:T(8,128)} %get-tuple-element.60), custom_call_target="Cholesky" | custom-call | tf_op jit(solution)/shard_map/jit(cholesky)/cholesky | solution.py:22
  251.3 2.1 fusion.33
  253.4 11.3 %custom-call.25 = f32[1,1,128,128]{2,3,1,0:T(8,128)} custom-call(f32[1,1,128,128]{3,2,1,0:T(8,128)} %fusion.33), custom_call_target="InvertDiagBlocksLowerTriangular" | custom-call | tf_op jit(solution)/shard_map/triangular_solve/custom-call.2 | solution.py:23
  266.8 4.1 convolution_bitcast_fusion.9
  270.9 13.2 %custom-call.22 = f32[1,128,128]{2,1,0:T(8,128)} custom-call(f32[1,128,128]{2,1,0:T(8,128)} %get-tuple-element.61), custom_call_target="Cholesky" | custom-call | tf_op jit(solution)/shard_map/jit(cholesky)/cholesky | solution.py:22
  285.6 2.1 fusion.32
  287.7 11.3 %custom-call.23 = f32[1,1,128,128]{2,3,1,0:T(8,128)} custom-call(f32[1,1,128,128]{3,2,1,0:T(8,128)} %fusion.32), custom_call_target="InvertDiagBlocksLowerTriangular" | custom-call | tf_op jit(solution)/shard_map/triangular_solve/custom-call.2 | solution.py:23
  300.4 1.9 fusion.29
  302.4 3.9 convolution_bitcast_fusion.12
  306.2 26.0 %custom-call.30 = f32[3,88,88]{2,1,0:T(8,128)} custom-call(f32[3,88,88]{2,1,0:T(8,128)} %get-tuple-element.57), custom_call_target="Cholesky" | custom-call | tf_op jit(solution)/shard_map/jit(cholesky)/cholesky | solution.py:22
  332.2 25.6 %custom-call.32 = f32[3,88,88]{2,1,0:T(8,128)} custom-call(f32[3,88,88]{2,1,0:T(8,128)} %get-tuple-element.56), custom_call_target="Cholesky" | custom-call | tf_op jit(solution)/shard_map/jit(cholesky)/cholesky | solution.py:22
  357.8 1.7 copy.81
  359.5 1.6 fusion.27
  361.1 25.6 %custom-call.34 = f32[3,88,88]{2,1,0:T(8,128)} custom-call(f32[3,88,88]{2,1,0:T(8,128)} %fusion.27), custom_call_target="Cholesky" | custom-call | tf_op jit(solution)/shard_map/jit(cholesky)/cholesky | solution.py:22
  388.2 1.9 select_bitcast_fusion
  390.0 21.7 %custom-call.35 = f32[3,1,88,88]{2,3,1,0:T(8,128)} custom-call(f32[3,1,88,88]{3,2,1,0:T(8,128)} %get-tuple-element.53), custom_call_target="InvertDiagBlocksLowerTriangular" | custom-call | tf_op jit(solution)/shard_map/triangular_solve/custom-call.3 | solution.py:23
  411.7 1.8 convolution_bitcast_fusion
  414.3 2.9 fusion.12
  417.3 21.9 %custom-call.33 = f32[3,1,88,88]{2,3,1,0:T(8,128)} custom-call(f32[3,1,88,88]{3,2,1,0:T(8,128)} %get-tuple-element.54), custom_call_target="InvertDiagBlocksLowerTriangular" | custom-call | tf_op jit(solution)/shard_map/triangular_solve/custom-call.3 | solution.py:23
  439.2 1.8 convolution_bitcast_fusion.1
  441.7 4.8 fusion.10
  446.5 21.7 %custom-call.31 = f32[3,1,88,88]{2,3,1,0:T(8,128)} custom-call(f32[3,1,88,88]{3,2,1,0:T(8,128)} %get-tuple-element.55), custom_call_target="InvertDiagBlocksLowerTriangular" | custom-call | tf_op jit(solution)/shard_map/triangular_solve/custom-call.3 | solution.py:23
  468.2 1.8 convolution_bitcast_fusion.2
  470.8 4.8 fusion.8
  476.8 5.8 %psum.223 = f32[3,1,88]{2,0,1:T(4,128)S(1)} all-reduce(f32[3,1,88]{2,0,1:T(4,128)S(1)} %bitcast.231), channel_id=1, replica_groups=mesh['layer'=2,'tp'=4,'fsdp'=4] {'fsdp'}, use_global_device_ids=true, to_apply=%region_38.43 | all-reduce | flops 264 | bytes 2112 | tf_op jit(solution)/shard_map/psum | solution.py:26
  483.8 5.2 multiply_subtract_fusion.1
  489.1 3.4 multiply_subtract_fusion
  492.5 31.4 %all-reduce.14.cloned.1.call-done = (f32[1,512,128]{2,1,0:T(8,128)}, f32[1,512,128]{2,1,0:T(8,128)}, f32[1,512,128]{2,1,0:T(8,128)}, f32[1,512,128]{2,1,0:T(8,12...) async-done(((f32[1,512,128]{2,1,0:T(8,128)}, f32[1,512,128]{2,1,0:T(8,128)}, f32[1,512,128]{2,1,0:T(8,128)}, f32[1,512,128]{2,1,0:T(8,128)}, f32[3,352,88]{1,2,0:T(8,128)}, ...) | async-done | bytes 1792016 | tf_op jit(solution)/shard_map/psum | solution.py:24
  525.1 5.7 multiply_subtract_fusion.2
  531.0 3.4 multiply_subtract_fusion.4
  534.5 2.1 fusion
  536.7 2.1 fusion.2
  538.9 2.1 fusion.4
  541.1 2.3 fusion.6
  543.4 12.0 %all-reduce.2 = (f32[1,1,128]{2,1,0:T(1,128)S(1)}, f32[1,1,128]{2,1,0:T(1,128)S(1)}, f32[1,1,128]{2,1,0:T(1,128)S(1)}, f32[1,1,128]{2,1,0:T(1,128)S(1)}, f32[3,1...) all-reduce(f32[1,1,128]{2,1,0:T(1,128)S(1)} %bitcast.235, ...), channel_id=1, replica_groups=mesh['layer'=2,'tp'=4,'fsdp'=4] {'tp'}, use_global_device_ids=true, to_apply=%region_6.9 | all-reduce | flops 1040 | bytes 8320 | tf_op jit(solution)/shard_map/psum | solution.py:26
  557.5 3.4 multiply_subtract_fusion.3
  560.9 3.3 multiply_subtract_fusion.5
  564.3 2.1 fusion.1
  566.4 2.1 fusion.3
  568.4 2.1 fusion.5
  570.5 2.1 fusion.7
  (210 shorter events, 33.7 us)
Async XLA Ops:
  7.2 105.3 %all-reduce.18.cloned.1.call-start = ((), (), s32[]{:S(2)}) async-start(), calls=%async_computation.4 | async-start | bytes 4259840 | tf_op jit(solution)/shard_map/psum | solution.py:20
  8.2 4.6 copy-start.3
  8.2 4.6 copy-start.6
  8.2 4.6 copy-start.68
  12.8 2.7 copy-start.12
  12.9 2.7 copy-start.27
  12.9 2.7 copy-start.71
  12.9 4.4 copy-start.14
  12.9 4.4 copy-start.29
  12.9 4.4 copy-start.72
  15.5 3.5 copy-start.8
  15.5 3.5 copy-start.23
  15.6 3.5 copy-start.73
  17.3 3.4 copy-start.10
  17.3 3.4 copy-start.25
  17.3 3.4 copy-start.74
  22.4 136.6 %all-reduce.16.cloned.1.call-start = ((), (), s32[]{:S(2)}) async-start(), calls=%async_computation.3 | async-start | bytes 2146304 | tf_op jit(solution)/shard_map/psum | solution.py:21
  112.5 5.1 copy-start.63
  112.5 6.3 %copy-start.62 = (f32[1,512,128]{2,1,0:T(8,128)S(1)}, f32[1,512,128]{2,1,0:T(8,128)}, u32[]{:S(2)}) copy-start(f32[1,512,128]{2,1,0:T(8,128)} %get-tuple-element.49) | copy-start | bytes 786436
  112.5 7.5 %copy-start.61 = (f32[1,512,128]{2,1,0:T(8,128)S(1)}, f32[1,512,128]{2,1,0:T(8,128)}, u32[]{:S(2)}) copy-start(f32[1,512,128]{2,1,0:T(8,128)} %get-tuple-element.48) | copy-start | bytes 786436
  112.5 8.8 %copy-start.60 = (f32[1,512,128]{2,1,0:T(8,128)S(1)}, f32[1,512,128]{2,1,0:T(8,128)}, u32[]{:S(2)}) copy-start(f32[1,512,128]{2,1,0:T(8,128)} %get-tuple-element.47) | copy-start | bytes 786436
  122.5 235.3 %all-reduce.10.cloned.1.call-start = ((), (), s32[]{:S(2)}) async-start(), calls=%async_computation | async-start | bytes 270336 | tf_op jit(solution)/shard_map/psum | solution.py:21
  159.1 8.2 %copy-start.69 = (f32[1,128,128]{1,2,0:T(8,128)S(1)}, f32[1,128,128]{1,2,0:T(8,128)}, u32[]{:S(2)}) copy-start(f32[1,128,128]{1,2,0:T(8,128)} %get-tuple-element.36) | copy-start | bytes 196612
  159.1 8.2 %copy-start.70 = (f32[1,128,128]{1,2,0:T(8,128)S(1)}, f32[1,128,128]{1,2,0:T(8,128)}, u32[]{:S(2)}) copy-start(f32[1,128,128]{1,2,0:T(8,128)} %get-tuple-element.37) | copy-start | bytes 196612
  165.0 310.7 %all-reduce.12.cloned.1.call-start = ((), (), s32[]{:S(2)}) async-start(), calls=%async_computation.1 | async-start | bytes 811008 | tf_op jit(solution)/shard_map/psum | solution.py:24
  417.3 106.6 %all-reduce.14.cloned.1.call-start = ((), (), s32[]{:S(2)}) async-start(), calls=%async_computation.2 | async-start | bytes 3719168 | tf_op jit(solution)/shard_map/psum | solution.py:24
  483.8 5.3 copy-start.53
  483.8 5.3 copy-start.22
  483.8 5.3 copy-start.43
  525.0 5.8 copy-start.40
  525.0 5.9 %copy-start.4 = (f32[3,512,352]{1,2,0:T(8,128)S(1)}, f32[3,512,352]{1,2,0:T(8,128)}, u32[]{:S(2)}) copy-start(f32[3,512,352]{1,2,0:T(8,128)} %param.51) | copy-start | bytes 6488068
  525.0 5.9 %copy-start.7 = (bf16[3,512,352]{1,2,0:T(8,128)(2,1)S(1)}, bf16[3,512,352]{1,2,0:T(8,128)(2,1)}, u32[]{:S(2)}) copy-start(bf16[3,512,352]{1,2,0:T(8,128)(2,1)} %param.52) | copy-start | bytes 3244036
  525.0 5.9 %copy-start.19 = (f32[3,512,88]{1,2,0:T(8,128)S(1)}, f32[3,512,88]{1,2,0:T(8,128)}, u32[]{:S(2)}) copy-start(f32[3,512,88]{1,2,0:T(8,128)} %copy-done.18) | copy-start | bytes 1622020
  530.9 3.4 copy-start.50
  531.0 3.5 copy-start.9
  531.0 3.5 copy-start.24
  534.4 2.3 copy-start.11
  534.4 2.3 copy-start.26
  534.4 2.3 copy-start.32
  536.6 2.3 copy-start.13
  536.6 2.3 copy-start.28
  536.6 2.3 copy-start.35
  538.8 2.3 copy-start.30
  538.8 2.3 copy-start.38
  541.0 14.5 %copy-start.42 = (f32[3,352,88]{1,2,0:T(8,128)S(1)}, f32[3,352,88]{1,2,0:T(8,128)}, u32[]{:S(2)}) copy-start(f32[3,352,88]{1,2,0:T(8,128)} %get-tuple-element.33) | copy-start | bytes 1115140
  541.0 14.7 %copy-start.41 = (f32[3,352,88]{1,2,0:T(8,128)S(1)}, f32[3,352,88]{1,2,0:T(8,128)}, u32[]{:S(2)}) copy-start(f32[3,352,88]{1,2,0:T(8,128)} %get-tuple-element.32) | copy-start | bytes 1115140
  543.4 13.9 %copy-start.49 = (f32[1,512,128]{2,1,0:T(8,128)S(1)}, f32[1,512,128]{2,1,0:T(8,128)}, u32[]{:S(2)}) copy-start(f32[1,512,128]{2,1,0:T(8,128)} %get-tuple-element.30) | copy-start | bytes 786436
  543.4 13.9 %copy-start.47 = (f32[1,512,128]{2,1,0:T(8,128)S(1)}, f32[1,512,128]{2,1,0:T(8,128)}, u32[]{:S(2)}) copy-start(f32[1,512,128]{2,1,0:T(8,128)} %get-tuple-element.29) | copy-start | bytes 786436
  543.4 14.0 %copy-start.45 = (f32[1,512,128]{2,1,0:T(8,128)S(1)}, f32[1,512,128]{2,1,0:T(8,128)}, u32[]{:S(2)}) copy-start(f32[1,512,128]{2,1,0:T(8,128)} %get-tuple-element.28) | copy-start | bytes 786436
  543.4 14.0 %copy-start.17 = (f32[3,512,88]{1,2,0:T(8,128)S(1)}, f32[3,512,88]{1,2,0:T(8,128)}, u32[]{:S(2)}) copy-start(f32[3,512,88]{1,2,0:T(8,128)} %copy-done.16) | copy-start | bytes 1622020
  555.6 5.2 copy-start.54
  555.8 5.1 copy-start.55
  557.3 7.0 %copy-start.56 = (f32[512,128]{1,0:T(8,128)}, f32[512,128]{1,0:T(8,128)S(1)}, u32[]{:S(2)}) copy-start(f32[512,128]{1,0:T(8,128)S(1)} %divide_bitcast_fusion) | copy-start | bytes 786436
  557.3 9.0 %copy-start.57 = (f32[512,128]{1,0:T(8,128)}, f32[512,128]{1,0:T(8,128)S(1)}, u32[]{:S(2)}) copy-start(f32[512,128]{1,0:T(8,128)S(1)} %divide_bitcast_fusion.1) | copy-start | bytes 786436
  557.4 11.0 %copy-start.58 = (f32[512,128]{1,0:T(8,128)}, f32[512,128]{1,0:T(8,128)S(1)}, u32[]{:S(2)}) copy-start(f32[512,128]{1,0:T(8,128)S(1)} %divide_bitcast_fusion.2) | copy-start | bytes 786436
  557.5 13.0 %copy-start.59 = (f32[512,128]{1,0:T(8,128)}, f32[512,128]{1,0:T(8,128)S(1)}, u32[]{:S(2)}) copy-start(f32[512,128]{1,0:T(8,128)S(1)} %divide_bitcast_fusion.3) | copy-start | bytes 786436
  557.5 3.4 copy-start.20
  557.5 3.4 copy-start.52
  560.9 3.3 copy-start.64
  564.2 4.2 copy-start.36
  564.2 4.2 copy-start.66
  566.3 4.2 copy-start.39
  566.3 4.2 copy-start.67
  566.4 6.2 %copy-start.1 = (f32[3,352,88]{1,2,0:T(8,128)S(1)}, f32[3,352,88]{1,2,0:T(8,128)}, u32[]{:S(2)}) copy-start(f32[3,352,88]{1,2,0:T(8,128)} %param.57) | copy-start | bytes 1115140
  (16 other events, 25.9 us)
Sparse Core Ops, SparseCore 0:
  22.6 89.9 all-reduce.17
  122.7 36.3 all-reduce.15
  165.1 35.5 all-reduce.9
  417.4 38.0 all-reduce.11
  475.8 48.0 all-reduce.13
where the time goes:
time: 587 us; the launch traced here: 580 us
  other arithmetic  266 us (45%)
  waiting for transfers between devices  154 us (26%)
  matrix products  110 us (19%)
  blocking collectives  17.9 us (3%)
  local copies, waits for them, and re-layouts  15.2 us (3%)
  between operations  15.1 us (3%)
    another operation x20, other arithmetic, dion_local(): chol_low = jnp.linalg.cholesky(gram_mat)  136 us
    another operation x13, other arithmetic, dion_local(): lax.linalg.triangular_solve(chol_low, p_tilde, left_side=False, lower=Tru...  118 us
    dot_general x35, matrix products, mat_mul(): jnp.einsum(form, left_op, right_op, preferred_element_type=jnp.float32, p...  99.6 us
    psum x1, waiting for transfers between devices, dion_local(): p_tilde = lax.psum(mat_mul(forms[0], mom_grad, factor), short_axis)  86.2 us
    psum x2, waiting for transfers between devices, dion_local(): gram_mat = lax.psum(mat_mul('bmr,bms->brs', p_tilde, p_tilde), long_axis)  36.4 us
    psum x2, waiting for transfers between devices, dion_local(): r_new = lax.psum(mat_mul(forms[1], mom_grad, p_orth), long_axis)  31.4 us
    psum x2, blocking collectives, dion_local(): col_sq = lax.psum(jnp.sum(r_new * r_new, axis=1, keepdims=True), short_axis)  17.9 us
  transfers between devices with their start and end apart: 5, of which 3 were waited for; matrix products, arithmetic and copies ran while one was open for 45% of the time, Pallas kernels for 0%

commit v1 on v0

v1 whole, which is shorter than its diff:
```python
import functools
import math
import jax
import jax.numpy as jnp
from jax import lax
from jax.experimental import pallas as pl
from jax.experimental.pallas import tpu as pltpu
from jax.sharding import PartitionSpec as P

MOMENTUM = 0.9
LEARN_RATE = 0.3
F32 = jnp.float32
BF16 = jnp.bfloat16
ND, NG, NE = 4, 6, 3
RD, RE, RX = 128, 96, 88
SQ, SN = 512, 352


def split3(x):
    hi = x.astype(BF16)
    rest = x - hi.astype(F32)
    mid = rest.astype(BF16)
    low = (rest - mid.astype(F32)).astype(BF16)
    return hi, mid, low


def dot(a, b, trans=False):
    dims = (((1,), (1 if trans else 0,)), ((), ()))
    return lax.dot_general(a, b, dims, preferred_element_type=F32)


def mm6(a3, r, b1, b2, b3, trans=False):
    o1 = dot(a3, b1, trans)
    o2 = dot(a3[:2 * r], b2, trans)
    o3 = dot(a3[:r], b3, trans)
    return o1[:r] + ((o1[r:2 * r] + o2[:r]) + ((o1[2 * r:] + o2[r:]) + o3))


def stack3(x):
    return jnp.concatenate(split3(x), axis=0)


def load_sum(m_ref, g_ref, bs_ref, k, rows):
    step = 32

    def body(c, carry):
        sl = pl.ds(pl.multiple_of(c * step, step), step)
        b = m_ref[k, sl, :] + g_ref[k, sl, :].astype(F32)
        b1, b2, b3 = split3(b)
        bs_ref[k, 0, sl, :] = b1
        bs_ref[k, 1, sl, :] = b2
        bs_ref[k, 2, sl, :] = b3
        return carry

    lax.fori_loop(0, rows // step, body, 0)


def sub_bcast(x, t):
    return jnp.broadcast_to(x[t:t + 1, :], (8, 128))


def chol_block(a_ref, li_ref, k, jb, rp):
    lane = lax.broadcasted_iota(jnp.int32, (8, 128), 1)
    sub = lax.broadcasted_iota(jnp.int32, (8, 128), 0)
    base = jb * 8
    row0 = pl.multiple_of(base, 8)
    panel = a_ref[k, pl.ds(row0, 8), :]
    cols = [jnp.take_along_axis(panel, jnp.full((8, 128), 0, jnp.int32) + (base + s), axis=1,
                                mode='promise_in_bounds') for s in range(8)]
    rinv = jnp.zeros((8, 128), F32)
    for t in range(8):
        d = sub_bcast(cols[t], t)
        inv = 1.0 / d
        rinv = jnp.where(sub == t, inv, rinv)
        mult = jnp.where(sub > t, cols[t] * inv, 0.0)
        for s in range(8):
            if s != t:
                cols[s] = cols[s] - mult * sub_bcast(cols[s], t)
        cols[t] = jnp.where(sub == t, 1.0, -mult)
    low = [jnp.where(sub >= s, cols[s], 0.0) for s in range(8)]
    rows = low[0] * sub_bcast(panel, 0)
    for s in range(1, 8):
        rows = rows + low[s] * sub_bcast(panel, s)
    for s in range(8):
        rows = jnp.where(lane == base + s, low[s], rows)
    scale = jnp.sqrt(rinv)
    li_ref[k, pl.ds(row0, 8), :] = jnp.where(lane < base + 8, rows * scale, 0.0)
    f = jnp.where(lane >= base + 8, rows * rinv, 0.0)
    f1, f2, f3 = [v.astype(F32) for v in split3(f)]
    r1, r2, r3 = [v.astype(F32) for v in split3(rows)]
    lhs = jnp.concatenate([f1, f1, f2, f2, f1, f3], axis=0)
    rhs = jnp.concatenate([r1, r2, r1, r2, r3, r1], axis=0)
    upd = lax.dot_general(lhs.T, rhs, (((1,), (0,)), ((), ())), preferred_element_type=F32)
    lane_all = lax.broadcasted_iota(jnp.int32, (rp, 128), 1)
    inside = (lane_all >= base) & (lane_all < base + 8)
    a_ref[k] = jnp.where(inside, 0.0, a_ref[k]) - upd[:rp]


def chol(a_ref, li_ref, ks, nblk, rp):
    def body(jb, carry):
        for k in ks:
            chol_block(a_ref, li_ref, k, jb, rp)
        return carry

    lax.fori_loop(0, nblk, body, 0)


def comm_kernel(*refs):
    names = [
        'md0', 'gd0', 'qd0', 'md1', 'gd1', 'qd1', 'md2', 'gd2', 'qd2', 'md3', 'gd3', 'qd3',
        'mga', 'gga', 'qga', 'mup', 'gup', 'qup', 'mdn', 'gdn', 'qdn',
        'po_d', 'po_g', 'po_n', 'rt_d', 'rt_g', 'rt_n', 'inv_t', 'inv_f',
        'Md', 'Gd', 'Qd', 'Mg', 'Gg', 'Qg', 'Mn', 'Gn', 'Qn', 'Bd', 'Bg', 'Bn',
        'pd', 'pdA', 'pdB', 'pdT', 'pg', 'pgA', 'pgB', 'pgT', 'vn', 'vnA', 'vnB', 'vnT',
        'yd', 'yd1', 'ydh', 'yd2', 'ydT', 'yg', 'yg1', 'ygh', 'yg2', 'ygT', 'yn', 'yn1', 'ynh', 'yn2', 'ynT',
        'Ad', 'Ld', 'Ag', 'Lg', 'An', 'Ln', 'st', 'sr', 'ft', 'fr',
        'lsem', 'zs_d', 'zr_d', 'zs_g', 'zr_g', 'zs_n', 'zr_n', 'ys_d', 'yr_d', 'ys_g', 'yr_g', 'ys_n', 'yr_n',
        'ns', 'nr', 'fs', 'fr2']
    v = dict(zip(names, refs))
    assert len(names) == len(refs)
    z = lax.axis_index('tp')
    f = lax.axis_index('fsdp')
    core = lax.rem(f, 2)
    outer = (z == 0) | (z == 3)
    inner = jnp.logical_not(outer)
    edge = z + 1 - 2 * lax.rem(z, 2)
    mid = 3 - z
    core_p = f + 1 - 2 * core
    y_p = lax.rem(f + 2, 4)

    def lcopy(src, dst, i, j):
        return pltpu.make_async_copy(src, dst, v['lsem'].at[i, j])

    loads = []
    for k in range(ND):
        loads.append([lcopy(v[f'md{k}'], v['Md'].at[k], 0, k), lcopy(v[f'gd{k}'], v['Gd'].at[k], 1, k),
                      lcopy(v[f'qd{k}'], v['Qd'].at[k], 2, k)])
    for e in range(NE):
        loads.append([lcopy(v['mdn'].at[e], v['Mn'].at[e], 0, ND + e), lcopy(v['gdn'].at[e], v['Gn'].at[e], 1, ND + e),
                      lcopy(v['qdn'].at[e], v['Qn'].at[e], 2, ND + e)])
    for k in range(NG):
        m, g, q = ('mga', 'gga', 'qga') if k < 3 else ('mup', 'gup', 'qup')
        loads.append([lcopy(v[m].at[k % 3], v['Mg'].at[k], 0, 7 + k), lcopy(v[g].at[k % 3], v['Gg'].at[k], 1, 7 + k),
                      lcopy(v[q].at[k % 3], v['Qg'].at[k], 2, 7 + k)])
    for group in loads:
        for c in group:
            c.start()

    barrier = pltpu.get_barrier_semaphore()
    for d in range(1, 4):
        pl.semaphore_signal(barrier, inc=1, device_id={'tp': lax.rem(z + d, 4)}, device_id_type=pl.DeviceIdType.MESH)
        pl.semaphore_signal(barrier, inc=1, device_id={'fsdp': lax.rem(f + d, 4)}, device_id_type=pl.DeviceIdType.MESH)
    pl.semaphore_wait(barrier, 6)

    def remote(src, dst, ssem, rsem, dev):
        return pltpu.make_async_remote_copy(src_ref=src, dst_ref=dst, send_sem=ssem, recv_sem=rsem,
                                            device_id=dev, device_id_type=pl.DeviceIdType.MESH)

    def zset(own, a, b, t, ss, rs, rows):
        own, a, b, t, ss, rs = v[own], v[a], v[b], v[t], v[ss], v[rs]

        def cut(ref, k):
            return ref.at[k, pl.ds(0, rows), :]

        def ca(k):
            return remote(cut(own, k), cut(a, k), ss.at[0, k], rs.at[0, k], {'tp': edge})

        def cb(k):
            return remote(cut(own, k), cut(b, k), ss.at[1, k], rs.at[1, k], {'tp': mid})

        def ct(k):
            return remote(cut(t, k), cut(t, k), ss.at[2, k], rs.at[2, k], {'tp': edge})

        def send(k):
            @pl.when(outer)
            def _():
                ca(k).start()

        def s(k):
            @pl.when(inner)
            def _():
                ca(k).wait_recv()
                own[k, :rows] = own[k, :rows] + a[k, :rows]
                cb(k).start()

        def tt(k):
            @pl.when(inner)
            def _():
                cb(k).wait_recv()
                t[k, :rows] = own[k, :rows] + b[k, :rows]
                ct(k).start()

        def w(k):
            @pl.when(outer)
            def _():
                ct(k).wait_recv()

        def fin(k):
            @pl.when(outer)
            def _():
                ca(k).wait_send()

            @pl.when(inner)
            def _():
                cb(k).wait_send()
                ct(k).wait_send()

        return send, s, tt, w, fin

    def yset(own, r1, h, r2, t, ss, rs, half):
        own, r1, h, r2, t, ss, rs = v[own], v[r1], v[h], v[r2], v[t], v[ss], v[rs]
        mine = pl.ds(pl.multiple_of(core * half, 8), half)
        theirs = pl.ds(pl.multiple_of((1 - core) * half, 8), half)

        def c1(k):
            return remote(own.at[k, theirs, :], r1.at[k], ss.at[0, k], rs.at[0, k], {'fsdp': core_p})

        def c2(k):
            return remote(h.at[k], r2.at[k], ss.at[1, k], rs.at[1, k], {'fsdp': y_p})

        def c3(k):
            return remote(t.at[k, mine, :], t.at[k, mine, :], ss.at[2, k], rs.at[2, k], {'fsdp': core_p})

        def y1(k):
            c1(k).start()

        def y2(k):
            c1(k).wait_recv()
            h[k] = own[k, mine, :] + r1[k]
            c2(k).start()

        def y3(k):
            c2(k).wait_recv()
            t[k, mine, :] = h[k] + r2[k]
            c3(k).start()

        def y4(k):
            remote(t.at[k, mine, :], t.at[k, theirs, :], ss.at[2, k], rs.at[2, k], {'fsdp': core_p}).wait_recv()

        def fin(k):
            c1(k).wait_send()
            c2(k).wait_send()
            c3(k).wait_send()

        return y1, y2, y3, y4, fin

    zd = zset('pd', 'pdA', 'pdB', 'pdT', 'zs_d', 'zr_d', RD)
    zg = zset('pg', 'pgA', 'pgB', 'pgT', 'zs_g', 'zr_g', RX)
    zn = zset('vn', 'vnA', 'vnB', 'vnT', 'zs_n', 'zr_n', RX)
    yd = yset('yd', 'yd1', 'ydh', 'yd2', 'ydT', 'ys_d', 'yr_d', RD // 2)
    yg = yset('yg', 'yg1', 'ygh', 'yg2', 'ygT', 'ys_g', 'yr_g', RE // 2)
    yn = yset('yn', 'yn1', 'ynh', 'yn2', 'ynT', 'ys_n', 'yr_n', RE // 2)

    def loop(n, body):
        def go(k, carry):
            body(k)
            return carry
        lax.fori_loop(0, n, go, 0)

    zero_rows = jnp.zeros((RE - RX, SQ), F32)

    def q_stack(q, rp):
        qt = q.T
        if rp != qt.shape[0]:
            qt = jnp.concatenate([qt, jnp.zeros((rp - qt.shape[0], qt.shape[1]), F32)], axis=0)
        return stack3(qt)

    def part_d(k):
        lcopy(v['md0'], v['Md'].at[k], 0, k).wait()
        lcopy(v['gd0'], v['Gd'].at[k], 1, k).wait()
        lcopy(v['qd0'], v['Qd'].at[k], 2, k).wait()
        load_sum(v['Md'], v['Gd'], v['Bd'], k, SQ)
        B = v['Bd']
        v['pd'][k] = mm6(q_stack(v['Qd'][k], RD), RD, B[k, 0], B[k, 1], B[k, 2], True)
        zd[0](k)

    def part_g(k):
        lcopy(v['mga'].at[0], v['Mg'].at[k], 0, 7 + k).wait()
        lcopy(v['gga'].at[0], v['Gg'].at[k], 1, 7 + k).wait()
        lcopy(v['qga'].at[0], v['Qg'].at[k], 2, 7 + k).wait()
        load_sum(v['Mg'], v['Gg'], v['Bg'], k, SQ)
        B = v['Bg']
        v['pg'][k] = mm6(q_stack(v['Qg'][k], RE), RE, B[k, 0], B[k, 1], B[k, 2], True)
        v['pgT'][k, RX:] = zero_rows
        zg[0](k)

    def part_n(k):
        lcopy(v['mdn'].at[0], v['Mn'].at[k], 0, 4 + k).wait()
        lcopy(v['gdn'].at[0], v['Gn'].at[k], 1, 4 + k).wait()
        lcopy(v['qdn'].at[0], v['Qn'].at[k], 2, 4 + k).wait()
        load_sum(v['Mn'], v['Gn'], v['Bn'], k, SN)
        B = v['Bn']
        v['yn'][k] = mm6(q_stack(v['Qn'][k], RE), RE, B[k, 0], B[k, 1], B[k, 2])
        yn[0](k)

    def gram(p3, rp):
        return mm6(p3, rp, p3[:rp], p3[rp:2 * rp], p3[2 * rp:], True)

    def post_d(k):
        zd[3](k)
        p3 = stack3(v['pdT'][k])
        B = v['Bd']
        v['yd'][k, :, :SQ] = mm6(p3, RD, B[k, 0], B[k, 1], B[k, 2])
        v['yd'][k, :, SQ:] = gram(p3, RD)
        yd[0](k)

    def post_g(k):
        zg[3](k)
        p3 = stack3(v['pgT'][k])
        B = v['Bg']
        v['yg'][k, :, :SN] = mm6(p3, RE, B[k, 0], B[k, 1], B[k, 2])
        v['yg'][k, :, SN:384] = jnp.zeros((RE, 384 - SN), F32)
        v['yg'][k, :, 384:384 + RE] = gram(p3, RE)
        v['yg'][k, :, 384 + RE:] = jnp.zeros((RE, 128 - RE), F32)
        yg[0](k)

    def post_n(k):
        yn[3](k)
        p3 = stack3(v['ynT'][k])
        B = v['Bn']
        v['vn'][k, :, :SN] = mm6(p3, RE, B[k, 0], B[k, 1], B[k, 2], True)
        v['vn'][k, :, SN:384] = jnp.zeros((RE, 384 - SN), F32)
        v['vn'][k, :, 384:384 + RE] = gram(p3, RE)
        v['vn'][k, :, 384 + RE:] = jnp.zeros((RE, 128 - RE), F32)
        v['vnT'][k, RX:] = zero_rows
        zn[0](k)

    def orth(l_ref, p_ref, y_ref, po, rt, k, r, rp, width):
        l3 = stack3(l_ref[k, :, :rp])
        q3 = stack3(p_ref[k])
        po[k] = mm6(l3, rp, q3[:rp], q3[rp:2 * rp], q3[2 * rp:])
        y3 = stack3(y_ref[k, :, :width])
        res = mm6(l3, rp, y3[:rp], y3[rp:2 * rp], y3[2 * rp:])
        rt[k] = res
        return jnp.sum(res * res, axis=1, keepdims=True)

    loop(ND, part_d)
    loop(NE, part_n)

    def ph3(k):
        part_g(k)

        @pl.when(k < ND)
        def _():
            zd[1](jnp.minimum(k, ND - 1))

        @pl.when((k >= 1) & (k <= ND))
        def _():
            zd[2](jnp.clip(k - 1, 0, ND - 1))
    loop(NG, ph3)
    loop(NE, yn[1])
    loop(NE, yn[2])
    loop(NE, post_n)

    def ph5(k):
        zg[1](k)

        @pl.when(k >= 1)
        def _():
            zg[2](jnp.maximum(k - 1, 0))

        @pl.when(k < ND)
        def _():
            post_d(jnp.minimum(k, ND - 1))
    loop(NG, ph5)
    zg[2](NG - 1)
    loop(NE, zn[1])
    loop(NE, zn[2])
    loop(ND, yd[1])
    loop(ND, yd[2])
    loop(NG, post_g)

    def take_d(k):
        yd[3](k)
        v['Ad'][k] = v['ydT'][k, :, SQ:]
    loop(ND, take_d)
    chol(v['Ad'], v['Ld'], range(ND), RD // 8, RD)
    loop(NG, yg[1])
    loop(NG, yg[2])

    def take_n(k):
        zn[3](k)
        v['An'][k] = v['vnT'][k, :, 384:]
        v['Ln'][k, RX:] = jnp.zeros((RE - RX, 128), F32)
    loop(NE, take_n)
    chol(v['An'], v['Ln'], range(NE), RX // 8, RE)

    def take_g(k):
        yg[3](k)
        v['Ag'][k] = v['ygT'][k, :, 384:]
        v['Lg'][k, RX:] = jnp.zeros((RE - RX, 128), F32)
    loop(NG, take_g)
    chol(v['Ag'], v['Lg'], range(NG), RX // 8, RE)

    lane_sq = lax.broadcasted_iota(jnp.int32, (128, 128), 1)
    v['st'][...] = jnp.zeros((128, 128), F32)
    v['ft'][...] = jnp.zeros((128, 128), F32)

    def put(ref, col, rp, lane):
        here = lax.broadcasted_iota(jnp.int32, (rp, 128), 1) == lane
        ref[:rp] = jnp.where(here, jnp.broadcast_to(col, (rp, 128)), ref[:rp])

    def orth_d(k):
        put(v['st'], orth(v['Ld'], v['pdT'], v['ydT'], v['po_d'], v['rt_d'], k, RD, RD, SQ), RD, k)
    loop(ND, orth_d)

    def orth_n(k):
        put(v['ft'], orth(v['Ln'], v['ynT'], v['vnT'], v['po_n'], v['rt_n'], k, RX, RE, SN), RE, k)
    loop(NE, orth_n)

    def orth_g(k):
        put(v['st'], orth(v['Lg'], v['pgT'], v['ygT'], v['po_g'], v['rt_g'], k, RX, RE, SN), RE, ND + k)
    loop(NG, orth_g)

    v['sr'][0] = v['st'][...].T[:16]
    v['fr'][0] = v['ft'][...].T[:16]
    copies = []
    for d in range(1, 4):
        copies.append(remote(v['sr'].at[0], v['sr'].at[d], v['ns'].at[d], v['nr'].at[d], {'tp': lax.rem(z + d, 4)}))
        copies.append(remote(v['fr'].at[0], v['fr'].at[d], v['fs'].at[d], v['fr2'].at[d], {'fsdp': lax.rem(f + d, 4)}))
    for c in copies:
        c.start()
    for c in copies:
        c.wait_recv()
    pad = jnp.zeros((112, 128), F32)
    tot_t = (v['sr'][0] + v['sr'][2]) + (v['sr'][1] + v['sr'][3])
    tot_f = (v['fr'][0] + v['fr'][2]) + (v['fr'][1] + v['fr'][3])
    inv_t = jnp.where(tot_t > 0.0, 1.0 / jnp.sqrt(tot_t), 0.0)
    inv_f = jnp.where(tot_f > 0.0, 1.0 / jnp.sqrt(tot_f), 0.0)
    v['inv_t'][...] = jnp.concatenate([inv_t, pad], axis=0).T
    v['inv_f'][...] = jnp.concatenate([inv_f, pad], axis=0).T

    for c in copies:
        c.wait_send()
    loop(ND, zd[4])
    loop(NG, zg[4])
    loop(NE, zn[4])
    loop(ND, yd[4])
    loop(NG, yg[4])
    loop(NE, yn[4])


def update_kernel(*refs):
    names = ['po_d', 'po_g', 'po_n', 'rt_d', 'rt_g', 'rt_n', 'inv_t', 'inv_f']
    ins = []
    for g in ('d0', 'd1', 'd2', 'd3', 'ga', 'up', 'dn'):
        ins += [f'x{g}', f'm{g}', f'g{g}']
    outs = []
    for g in ('d0', 'd1', 'd2', 'd3', 'ga', 'up', 'dn'):
        outs += [f'X{g}', f'M{g}', f'Q{g}']
    scr = ['xd', 'md', 'gd', 'xg', 'mg', 'gg', 'xn', 'mn', 'gn', 'lsem', 'osem']
    v = dict(zip(names + ins + outs + scr, refs))
    assert len(names + ins + outs + scr) == len(refs)
    tags = [('d0', None), ('d1', None), ('d2', None), ('d3', None)] + [('ga', e) for e in range(3)] + \
        [('up', e) for e in range(3)] + [('dn', e) for e in range(3)]

    def at(name, e):
        return v[name] if e is None else v[name].at[e]

    def slot(i):
        if i < 4:
            return 'd', i
        if i < 10:
            return 'g', i - 4
        return 'n', i - 10

    loads, stores = [], []
    for i, (tag, e) in enumerate(tags):
        g, k = slot(i)
        loads.append([pltpu.make_async_copy(at(c + tag, e), v[c + g].at[k], v['lsem'].at[j, i])
                      for j, c in enumerate(('m', 'g', 'x'))])
        stores.append([pltpu.make_async_copy(v[c.lower() + g].at[k], at(c + tag, e), v['osem'].at[j, i])
                       for j, c in enumerate(('M', 'X'))])
    for group in loads:
        for c in group:
            c.start()

    def pack(x):
        a, b, c = split3(x)
        return jnp.concatenate([a, b], axis=1), jnp.concatenate([a, c], axis=1)

    def packs(y):
        a, b, c = split3(y)
        return (jnp.concatenate([a, b], axis=0), jnp.concatenate([b, a], axis=0), jnp.concatenate([c, a], axis=0))

    def pad(x):
        if x.shape[0] == 128:
            return x
        return jnp.concatenate([x, jnp.zeros((128 - x.shape[0], x.shape[1]), F32)], axis=0)

    def prod(lhs, rhs):
        return dot(lhs[0], rhs[0]) + (dot(lhs[0], rhs[1]) + dot(lhs[1], rhs[2]))

    for i, (tag, e) in enumerate(tags):
        g, k = slot(i)
        pt = pad(v['po_' + g][k])
        rt = pad(v['rt_' + g][k])
        inv = v['inv_f'][:, k:k + 1] if g == 'n' else v['inv_t'][:, i:i + 1]
        qt = rt * jnp.broadcast_to(inv, rt.shape)
        flip = g == 'n'
        for c in loads[i]:
            c.wait()
        m, gr, x = v['m' + g], v['g' + g], v['x' + g]
        eta = LEARN_RATE * (math.sqrt(2048 / 1408) if i >= 4 else 1.0)
        if flip:
            q = qt.T
            rhs = packs(pt)
            m[k] = m[k] + gr[k].astype(F32) - (1.0 - MOMENTUM) * prod(pack(rt.T), rhs)
            stores[i][0].start()
            x[k] = x[k] - eta * prod(pack(q), rhs)
            stores[i][1].start()
        else:
            lhs = pack(pt.T)
            m[k] = m[k] + gr[k].astype(F32) - (1.0 - MOMENTUM) * prod(lhs, packs(rt))
            stores[i][0].start()
            x[k] = x[k] - eta * prod(lhs, packs(qt))
            stores[i][1].start()
            q = qt.T
        if e is None:
            v['Q' + tag][...] = q
        else:
            v['Q' + tag][e] = q[:, :RX]
    for group in stores:
        for c in group:
            c.wait()


def vm(*shape, dtype=F32):
    return pltpu.VMEM(shape, dtype)


def solution(mesh):
    dense_w = P(('layer', 'fsdp'), 'tp')
    dense_f = P(('layer', 'tp'), None)
    stack_w = P('layer', 'fsdp', 'tp')
    stack_f = P('layer', 'tp', None)
    down_f = P('layer', 'fsdp', None)
    in_specs = (dense_w, dense_w, dense_w, dense_f) * 4 + (stack_w, stack_w, stack_w, stack_f) * 2 + (stack_w, stack_w, stack_w, down_f)
    out_specs = (dense_w, dense_w, dense_f) * 4 + (stack_w, stack_w, stack_f) * 2 + (stack_w, stack_w, down_f)
    dma = pltpu.SemaphoreType.DMA
    anyspec = pl.BlockSpec(memory_space=pl.ANY)
    vspec = pl.BlockSpec(memory_space=pltpu.VMEM)

    def local_step(*blocks):
        mats = [blocks[4 * i:4 * i + 4] for i in range(7)]
        first = []
        for x, m, g, q in mats:
            first += [m, g, q]
        scratch = [
            vm(ND, SQ, SQ), vm(ND, SQ, SQ, dtype=BF16), vm(ND, SQ, RD),
            vm(NG, SQ, SN), vm(NG, SQ, SN, dtype=BF16), vm(NG, SN, RX),
            vm(NE, SN, SQ), vm(NE, SN, SQ, dtype=BF16), vm(NE, SN, RX),
            vm(ND, 3, SQ, SQ, dtype=BF16), vm(NG, 3, SQ, SN, dtype=BF16), vm(NE, 3, SN, SQ, dtype=BF16)]
        scratch += [vm(ND, RD, SQ)] * 4 + [vm(NG, RE, SQ)] * 4 + [vm(NE, RE, SQ)] * 4
        for n, rp, w in ((ND, RD, SQ + 128), (NG, RE, 512), (NE, RE, 512)):
            scratch += [vm(n, rp, w), vm(n, rp // 2, w), vm(n, rp // 2, w), vm(n, rp // 2, w), vm(n, rp, w)]
        for n, rp in ((ND, RD), (NG, RE), (NE, RE)):
            scratch += [vm(n, rp, 128), vm(n, rp, 128)]
        scratch += [vm(128, 128), vm(4, 16, 128), vm(128, 128), vm(4, 16, 128)]
        scratch += [dma((3, 13))]
        scratch += [dma((3, n)) for n in (ND, ND, NG, NG, NE, NE)] * 2
        scratch += [dma((4,))] * 4
        shapes = [(ND, RD, SQ), (NG, RE, SQ), (NE, RE, SQ), (ND, RD, SQ), (NG, RE, SN), (NE, RE, SN), (128, 128), (128, 128)]
        mids = pl.pallas_call(
            comm_kernel,
            out_shape=[jax.ShapeDtypeStruct(s, F32) for s in shapes],
            in_specs=[anyspec] * 21,
            out_specs=[vspec] * 8,
            scratch_shapes=scratch,
            name='comm',
            compiler_params=pltpu.CompilerParams(collective_id=0, has_side_effects=True, vmem_limit_bytes=64 * 1024 * 1024 - 65536),
        )(*first)
        second, shapes2, ospecs = [], [], []
        for x, m, g, q in mats:
            second += [x, m, g]
            shapes2 += [x, m, q]
            ospecs += [anyspec, anyspec, vspec]
        res = pl.pallas_call(
            update_kernel,
            out_shape=[jax.ShapeDtypeStruct(a.shape, F32) for a in shapes2],
            in_specs=[vspec] * 8 + [anyspec] * 21,
            out_specs=ospecs,
            scratch_shapes=[vm(ND, SQ, SQ), vm(ND, SQ, SQ), vm(ND, SQ, SQ, dtype=BF16),
                            vm(NG, SQ, SN), vm(NG, SQ, SN), vm(NG, SQ, SN, dtype=BF16),
                            vm(NE, SN, SQ), vm(NE, SN, SQ), vm(NE, SN, SQ, dtype=BF16), dma((3, 13)), dma((2, 13))],
            name='update',
            compiler_params=pltpu.CompilerParams(vmem_limit_bytes=64 * 1024 * 1024 - 65536),
        )(*mids, *second)
        return tuple(res)

    return jax.shard_map(local_step, mesh=mesh, in_specs=in_specs, out_specs=out_specs, check_vma=False)
```

time: 587 us -> 248 us (0.42); the launches traced: 580 us -> 247 us
  other arithmetic: 266 us -> 0 us
  Pallas kernels: 0 us -> 212 us
  waiting for transfers between devices: 154 us -> 0 us
  matrix products: 110 us -> 0 us
  local copies, waits for them, and re-layouts: 15.2 us -> 34.2 us
  blocking collectives: 17.9 us -> 0 us
  between operations: 15.1 us -> 0.71 us
    another operation x37 -> x0, other arithmetic: 256 us -> none  [the longest x20 136 us: dion_local(): chol_low = jnp.linalg.cholesky(gram_mat)]
    pallas_call x0 -> x2, Pallas kernels: none -> 212 us  [the longest x1 191 us: local_step(): pl.pallas_call(comm_kernel, out_shape=[jax.ShapeDtypeStruct(s, F32) for s...]
    psum x5 -> x0, waiting for transfers between devices: 154 us -> none  [the longest x1 86.2 us: dion_local(): p_tilde = lax.psum(mat_mul(forms[0], mom_grad, factor), short_axis)]
    dot_general x35 -> x0, matrix products: 99.6 us -> none  [mat_mul(): jnp.einsum(form, left_op, right_op, preferred_element_type=jnp.float32, p...]
    psum x2 -> x0, blocking collectives: 17.9 us -> none  [dion_local(): col_sq = lax.psum(jnp.sum(r_new * r_new, axis=1, keepdims=True), short_axis)]
    pallas_call x0 -> x7, local copies, waits for them, and re-layouts: none -> 15.1 us  [local_step(): pl.pallas_call(update_kernel, out_shape=[jax.ShapeDtypeStruct(a.shape, F3...]
    unnamed x150 -> x23, local copies, waits for them, and re-layouts: 5.07 us -> 19 us
    another operation x7 -> x0, matrix products: 10.9 us -> none  [dion_local(): lax.linalg.triangular_solve(chol_low, p_tilde, left_side=False, lower=Tru...]
  transfers between devices with their start and end apart: 5 -> 0, of which waited for: 3 -> 0; matrix products, arithmetic and copies ran while one was open for 45% -> 0% of each run, Pallas kernels for 0% -> 0%
where the time goes in v1:
time: 248 us; the launch traced here: 247 us
  Pallas kernels  212 us (85%)
  local copies, waits for them, and re-layouts  34.2 us (14%)
    pallas_call x1, Pallas kernels, local_step(): pl.pallas_call(comm_kernel, out_shape=[jax.ShapeDtypeStruct(s, F32) for s...  191 us
    pallas_call x1, Pallas kernels, local_step(): pl.pallas_call(update_kernel, out_shape=[jax.ShapeDtypeStruct(a.shape, F3...  21.7 us
    unnamed x23, local copies, waits for them, and re-layouts  19 us
    pallas_call x7, local copies, waits for them, and re-layouts, local_step(): pl.pallas_call(update_kernel, out_shape=[jax.ShapeDtypeStruct(a.shape, F3...  15.1 us

profile of v1, /device:TPU:0, one launch (start us, length us, event | category | flops | bytes accessed | tf_op | source)
XLA Modules:
  0.0 247.3 jit_solution(16573414338442849394)
XLA Ops:
  0.7 0.0 copy-start.6
  0.7 0.0 copy-start.4
  0.7 2.1 copy.51.refs_14_
  2.8 2.0 copy.54.refs_17_
  4.8 0.0 copy-done.6
  4.8 1.0 copy.55.refs_20_
  5.9 0.0 copy-done.4
  5.9 0.0 copy-start.2
  5.9 1.4 copy.50.refs_13_.refs_22_
  7.3 2.4 copy.53.refs_16_.refs_25_
  9.6 0.0 copy-done.2
  9.6 1.9 copy.49.refs_12_.refs_21_
  11.5 0.0 copy-start.3
  11.5 3.2 %copy.52.refs_15_.refs_24_ = f32[3,512,352]{2,1,0:T(8,128)} copy(f32[3,512,352]{1,2,0:T(8,128)} %param.49) | data formatting | bytes 4325376 | tf_op args[21]
  14.7 0.0 copy-done.3
  14.7 1.9 copy.56.refs_20_
  16.7 3.0 %copy.59.refs_23_ = f32[3,512,352]{2,1,0:T(8,128)} copy(f32[3,512,352]{1,2,0:T(8,128)} %param.48) | data formatting | bytes 4325376 | tf_op args[20]
  19.7 190.7 %comm.1 = (f32[4,128,512]{2,1,0:T(8,128)}, f32[6,96,512]{2,1,0:T(8,128)}, f32[3,96,512]{2,1,0:T(8,128)}, f32[4,128,512]{2,1,0:T(8,128)}, f32[6,96,352]{2,1,0:T(8...) custom-call(f32[512,512]{1,0:T(8,128)} %refs_9_.3, bf16[512,512]{1,0:T(8,128)(2,1)} %refs_10_.3, ...), custom_call_target="tpu_custom_call" | custom-call | tf_op jit(solution)/shard_map/comm/pallas_call | solution.py:564
  210.4 21.7 %update.1 = (f32[512,512]{1,0:T(8,128)}, f32[512,512]{1,0:T(8,128)}, f32[512,128]{1,0:T(8,128)}, f32[512,512]{1,0:T(8,128)}, f32[512,512]{1,0:T(8,128)}, /*index...) custom-call(f32[4,128,512]{2,1,0:T(8,128)} %get-tuple-element.29.ref, ...), custom_call_target="tpu_custom_call" | custom-call | tf_op jit(solution)/shard_map/update/pallas_call | solution.py:578
  232.1 0.0 copy-start.5
  232.1 2.1 copy.64
  234.2 2.0 copy.67
  236.2 0.0 copy-done.5
  236.2 1.0 copy.68
  237.2 0.0 copy-start.1
  237.2 3.1 %copy.62 = f32[3,512,352]{1,2,0:T(8,128)} copy(f32[3,512,352]{2,1,0:T(8,128)} %get-tuple-element.49) | data formatting | bytes 4325376 | tf_op jit(solution)/shard_map/update/pallas_call | solution.py:578
  240.4 0.0 copy-done.1
  240.4 1.9 copy.63
  242.2 0.0 copy-start
  242.2 3.1 %copy.65 = f32[3,512,352]{1,2,0:T(8,128)} copy(f32[3,512,352]{2,1,0:T(8,128)} %get-tuple-element.52) | data formatting | bytes 4325376 | tf_op jit(solution)/shard_map/update/pallas_call | solution.py:578
  245.4 0.0 copy-done
  245.4 1.9 copy.66
Async XLA Ops:
  0.7 4.2 %copy-start.6 = (f32[3,352,88]{1,2,0:T(8,128)S(1)}, f32[3,352,88]{1,2,0:T(8,128)}, u32[]{:S(2)}) copy-start(f32[3,352,88]{1,2,0:T(8,128)} %param.55) | copy-start | bytes 1115140
  0.7 5.2 %copy-start.4 = (bf16[3,512,352]{1,2,0:T(8,128)(2,1)S(1)}, bf16[3,512,352]{1,2,0:T(8,128)(2,1)}, u32[]{:S(2)}) copy-start(bf16[3,512,352]{1,2,0:T(8,128)(2,1)} %param.46) | copy-start | bytes 3244036
  5.9 3.8 %copy-start.2 = (f32[3,512,352]{1,2,0:T(8,128)S(1)}, f32[3,512,352]{1,2,0:T(8,128)}, u32[]{:S(2)}) copy-start(f32[3,512,352]{1,2,0:T(8,128)} %param.45) | copy-start | bytes 6488068
  11.5 3.2 %copy-start.3 = (f32[3,512,352]{1,2,0:T(8,128)S(1)}, f32[3,512,352]{1,2,0:T(8,128)}, u32[]{:S(2)}) copy-start(f32[3,512,352]{1,2,0:T(8,128)} %param.44) | copy-start | bytes 6488068
  232.1 4.1 %copy-start.5 = (f32[3,352,88]{2,1,0:T(8,128)S(1)}, f32[3,352,88]{2,1,0:T(8,128)}, u32[]{:S(2)}) copy-start(f32[3,352,88]{2,1,0:T(8,128)} %get-tuple-element.57) | copy-start | bytes 1115140
  237.2 3.1 %copy-start.1 = (f32[3,512,352]{2,1,0:T(8,128)S(1)}, f32[3,512,352]{2,1,0:T(8,128)}, u32[]{:S(2)}) copy-start(f32[3,512,352]{2,1,0:T(8,128)} %get-tuple-element.50) | copy-start | bytes 6488068
  242.2 3.1 %copy-start = (f32[3,512,352]{2,1,0:T(8,128)S(1)}, f32[3,512,352]{2,1,0:T(8,128)}, u32[]{:S(2)}) copy-start(f32[3,512,352]{2,1,0:T(8,128)} %get-tuple-element.53) | copy-start | bytes 6488068

commit v2 on v1

--- a/solution.py
+++ b/solution.py
@@ -9,6 +9,7 @@
 
 MOMENTUM = 0.9
 LEARN_RATE = 0.3
+VMEM_MAX = 58 * 1024 * 1024
 F32 = jnp.float32
 BF16 = jnp.bfloat16
 ND, NG, NE = 4, 6, 3
@@ -59,47 +60,56 @@
     return jnp.broadcast_to(x[t:t + 1, :], (8, 128))
 
 
-def chol_block(a_ref, li_ref, k, jb, rp):
+def chol_step(a_ref, li_ref, ks, jb, rp):
     lane = lax.broadcasted_iota(jnp.int32, (8, 128), 1)
     sub = lax.broadcasted_iota(jnp.int32, (8, 128), 0)
     base = jb * 8
     row0 = pl.multiple_of(base, 8)
-    panel = a_ref[k, pl.ds(row0, 8), :]
-    cols = [jnp.take_along_axis(panel, jnp.full((8, 128), 0, jnp.int32) + (base + s), axis=1,
-                                mode='promise_in_bounds') for s in range(8)]
-    rinv = jnp.zeros((8, 128), F32)
+    n = range(len(ks))
+    panel = [a_ref[k, pl.ds(row0, 8), :] for k in ks]
+    idx = [jnp.full((8, 128), 0, jnp.int32) + (base + s) for s in range(8)]
+    cols = [[jnp.take_along_axis(panel[i], idx[s], axis=1, mode='promise_in_bounds') for s in range(8)] for i in n]
+    rinv = [jnp.zeros((8, 128), F32) for i in n]
     for t in range(8):
-        d = sub_bcast(cols[t], t)
-        inv = 1.0 / d
-        rinv = jnp.where(sub == t, inv, rinv)
-        mult = jnp.where(sub > t, cols[t] * inv, 0.0)
+        inv = [1.0 / sub_bcast(cols[i][t], t) for i in n]
+        for i in n:
+            rinv[i] = jnp.where(sub == t, inv[i], rinv[i])
+        mult = [jnp.where(sub > t, cols[i][t] * inv[i], 0.0) for i in n]
+        for i in n:
+            for s in range(8):
+                if s != t:
+                    cols[i][s] = cols[i][s] - mult[i] * sub_bcast(cols[i][s], t)
+            cols[i][t] = jnp.where(sub == t, 1.0, -mult[i])
+    low = [[jnp.where(sub >= s, cols[i][s], 0.0) for s in range(8)] for i in n]
+    rows = []
+    for i in n:
+        r = low[i][0] * sub_bcast(panel[i], 0)
+        for s in range(1, 8):
+            r = r + low[i][s] * sub_bcast(panel[i], s)
         for s in range(8):
-            if s != t:
-                cols[s] = cols[s] - mult * sub_bcast(cols[s], t)
-        cols[t] = jnp.where(sub == t, 1.0, -mult)
-    low = [jnp.where(sub >= s, cols[s], 0.0) for s in range(8)]
-    rows = low[0] * sub_bcast(panel, 0)
-    for s in range(1, 8):
-        rows = rows + low[s] * sub_bcast(panel, s)
-    for s in range(8):
-        rows = jnp.where(lane == base + s, low[s], rows)
-    scale = jnp.sqrt(rinv)
-    li_ref[k, pl.ds(row0, 8), :] = jnp.where(lane < base + 8, rows * scale, 0.0)
-    f = jnp.where(lane >= base + 8, rows * rinv, 0.0)
-    f1, f2, f3 = [v.astype(F32) for v in split3(f)]
-    r1, r2, r3 = [v.astype(F32) for v in split3(rows)]
-    lhs = jnp.concatenate([f1, f1, f2, f2, f1, f3], axis=0)
-    rhs = jnp.concatenate([r1, r2, r1, r2, r3, r1], axis=0)
-    upd = lax.dot_general(lhs.T, rhs, (((1,), (0,)), ((), ())), preferred_element_type=F32)
+            r = jnp.where(lane == base + s, low[i][s], r)
+        rows.append(r)
+    upd = []
+    for i in n:
+        f = jnp.where(lane >= base + 8, rows[i] * rinv[i], 0.0)
+        f1, f2, f3 = [x.astype(F32) for x in split3(f)]
+        r1, r2, r3 = [x.astype(F32) for x in split3(rows[i])]
+        lhs = jnp.concatenate([f1, f1, f2, f2, f1, f3], axis=0)
+        rhs = jnp.concatenate([r1, r2, r1, r2, r3, r1], axis=0)
+        upd.append(lax.dot_general(lhs.T, rhs, (((1,), (0,)), ((), ())), preferred_element_type=F32))
     lane_all = lax.broadcasted_iota(jnp.int32, (rp, 128), 1)
     inside = (lane_all >= base) & (lane_all < base + 8)
-    a_ref[k] = jnp.where(inside, 0.0, a_ref[k]) - upd[:rp]
-
-
-def chol(a_ref, li_ref, ks, nblk, rp):
+    for i in n:
+        a_ref[ks[i]] = jnp.where(inside, 0.0, a_ref[ks[i]]) - upd[i][:rp]
+    for i in n:
+        li_ref[ks[i], pl.ds(row0, 8), :] = jnp.where(lane < base + 8, rows[i] * jnp.sqrt(rinv[i]), 0.0)
+
+
+def chol(a_ref, li_ref, ks, nblk, rp, duties=()):
     def body(jb, carry):
-        for k in ks:
-            chol_block(a_ref, li_ref, k, jb, rp)
+        chol_step(a_ref, li_ref, ks, jb, rp)
+        for at, duty in duties:
+            pl.when(jb == at)(duty)
         return carry
 
     lax.fori_loop(0, nblk, body, 0)
@@ -111,8 +121,8 @@
         'mga', 'gga', 'qga', 'mup', 'gup', 'qup', 'mdn', 'gdn', 'qdn',
         'po_d', 'po_g', 'po_n', 'rt_d', 'rt_g', 'rt_n', 'inv_t', 'inv_f',
         'Md', 'Gd', 'Qd', 'Mg', 'Gg', 'Qg', 'Mn', 'Gn', 'Qn', 'Bd', 'Bg', 'Bn',
-        'pd', 'pdA', 'pdB', 'pdT', 'pg', 'pgA', 'pgB', 'pgT', 'vn', 'vnA', 'vnB', 'vnT',
-        'yd', 'yd1', 'ydh', 'yd2', 'ydT', 'yg', 'yg1', 'ygh', 'yg2', 'ygT', 'yn', 'yn1', 'ynh', 'yn2', 'ynT',
+        'pd', 'pdT', 'pdB', 'pg', 'pgT', 'pgB', 'vn', 'vnT', 'vnB',
+        'yd', 'yd1', 'yd2', 'ydT', 'yg', 'yg1', 'yg2', 'ygT', 'yn', 'yn1', 'yn2', 'ynT',
         'Ad', 'Ld', 'Ag', 'Lg', 'An', 'Ln', 'st', 'sr', 'ft', 'fr',
         'lsem', 'zs_d', 'zr_d', 'zs_g', 'zr_g', 'zs_n', 'zr_n', 'ys_d', 'yr_d', 'ys_g', 'yr_g', 'ys_n', 'yr_n',
         'ns', 'nr', 'fs', 'fr2']
@@ -156,59 +166,55 @@
         return pltpu.make_async_remote_copy(src_ref=src, dst_ref=dst, send_sem=ssem, recv_sem=rsem,
                                             device_id=dev, device_id_type=pl.DeviceIdType.MESH)
 
-    def zset(own, a, b, t, ss, rs, rows):
-        own, a, b, t, ss, rs = v[own], v[a], v[b], v[t], v[ss], v[rs]
-
-        def cut(ref, k):
-            return ref.at[k, pl.ds(0, rows), :]
-
-        def ca(k):
-            return remote(cut(own, k), cut(a, k), ss.at[0, k], rs.at[0, k], {'tp': edge})
-
-        def cb(k):
-            return remote(cut(own, k), cut(b, k), ss.at[1, k], rs.at[1, k], {'tp': mid})
-
-        def ct(k):
-            return remote(cut(t, k), cut(t, k), ss.at[2, k], rs.at[2, k], {'tp': edge})
-
-        def send(k):
+    def zpiece(own, t, b, ss, rs, i, k, row0, rows, col0, cols):
+        own, t, b = [v[x].at[k, pl.ds(row0, rows), pl.ds(col0, cols)] for x in (own, t, b)]
+        ss, rs = v[ss], v[rs]
+        def ca():
+            return remote(own, t, ss.at[0, i], rs.at[0, i], {'tp': edge})
+        def cb():
+            return remote(own, b, ss.at[1, i], rs.at[1, i], {'tp': mid})
+        def ct():
+            return remote(t, t, ss.at[2, i], rs.at[2, i], {'tp': edge})
+
+        def send():
             @pl.when(outer)
             def _():
-                ca(k).start()
-
-        def s(k):
+                ca().start()
+
+        def half():
             @pl.when(inner)
             def _():
-                ca(k).wait_recv()
-                own[k, :rows] = own[k, :rows] + a[k, :rows]
-                cb(k).start()
-
-        def tt(k):
+                ca().wait_recv()
+                own[...] = own[...] + t[...]
+                cb().start()
+
+        def total():
             @pl.when(inner)
             def _():
-                cb(k).wait_recv()
-                t[k, :rows] = own[k, :rows] + b[k, :rows]
-                ct(k).start()
-
-        def w(k):
+                cb().wait_recv()
+                t[...] = own[...] + b[...]
+                ct().start()
+
+        def take():
             @pl.when(outer)
             def _():
-                ct(k).wait_recv()
-
-        def fin(k):
+                ct().wait_recv()
+
+        def done():
             @pl.when(outer)
             def _():
-                ca(k).wait_send()
+                ca().wait_send()
 
             @pl.when(inner)
             def _():
-                cb(k).wait_send()
-                ct(k).wait_send()
-
-        return send, s, tt, w, fin
-
-    def yset(own, r1, h, r2, t, ss, rs, half):
-        own, r1, h, r2, t, ss, rs = v[own], v[r1], v[h], v[r2], v[t], v[ss], v[rs]
+                cb().wait_send()
+                ct().wait_send()
+
+        return send, half, total, take, done
+
+    def yset(own, r1, r2, t, ss, rs, half):
+        own, r1, r2, t, ss, rs = v[own], v[r1], v[r2], v[t], v[ss], v[rs]
+        h = r1
         mine = pl.ds(pl.multiple_of(core * half, 8), half)
         theirs = pl.ds(pl.multiple_of((1 - core) * half, 8), half)
 
@@ -244,12 +250,38 @@
 
         return y1, y2, y3, y4, fin
 
-    zd = zset('pd', 'pdA', 'pdB', 'pdT', 'zs_d', 'zr_d', RD)
-    zg = zset('pg', 'pgA', 'pgB', 'pgT', 'zs_g', 'zr_g', RX)
-    zn = zset('vn', 'vnA', 'vnB', 'vnT', 'zs_n', 'zr_n', RX)
-    yd = yset('yd', 'yd1', 'ydh', 'yd2', 'ydT', 'ys_d', 'yr_d', RD // 2)
-    yg = yset('yg', 'yg1', 'ygh', 'yg2', 'ygT', 'ys_g', 'yr_g', RE // 2)
-    yn = yset('yn', 'yn1', 'ynh', 'yn2', 'ynT', 'ys_n', 'yr_n', RE // 2)
+    Z = []
+    where = {}
+    for k in range(ND):
+        for h in range(2):
+            where['d', k, h] = len(Z)
+            Z.append(zpiece('pd', 'pdT', 'pdB', 'zs_d', 'zr_d', 2 * k + h, k, h * 64, 64, 0, SQ))
+    for k in range(NE):
+        where['G', k] = len(Z)
+        Z.append(zpiece('vn', 'vnT', 'vnB', 'zs_n', 'zr_n', k, k, 0, RX, 384, 128))
+    for k in range(NG):
+        where['g', k] = len(Z)
+        Z.append(zpiece('pg', 'pgT', 'pgB', 'zs_g', 'zr_g', k, k, 0, RX, 0, SQ))
+    for k in range(NE):
+        where['Y', k] = len(Z)
+        Z.append(zpiece('vn', 'vnT', 'vnB', 'zs_n', 'zr_n', NE + k, k, 0, RX, 0, 384))
+
+
+    def A(*key):
+        Z[where[key]][0]()
+
+    def S(n):
+        Z[n][1]()
+
+    def T(n):
+        Z[n][2]()
+
+    def W(*key):
+        Z[where[key]][3]()
+
+    yd = yset('yd', 'yd1', 'yd2', 'ydT', 'ys_d', 'yr_d', RD // 2)
+    yg = yset('yg', 'yg1', 'yg2', 'ygT', 'ys_g', 'yr_g', RE // 2)
+    yn = yset('yn', 'yn1', 'yn2', 'ynT', 'ys_n', 'yr_n', RE // 2)
 
     def loop(n, body):
         def go(k, carry):
@@ -259,8 +291,7 @@
 
     zero_rows = jnp.zeros((RE - RX, SQ), F32)
 
-    def q_stack(q, rp):
-        qt = q.T
+    def q_stack(qt, rp):
         if rp != qt.shape[0]:
             qt = jnp.concatenate([qt, jnp.zeros((rp - qt.shape[0], qt.shape[1]), F32)], axis=0)
         return stack3(qt)
@@ -271,18 +302,18 @@
         lcopy(v['qd0'], v['Qd'].at[k], 2, k).wait()
         load_sum(v['Md'], v['Gd'], v['Bd'], k, SQ)
         B = v['Bd']
-        v['pd'][k] = mm6(q_stack(v['Qd'][k], RD), RD, B[k, 0], B[k, 1], B[k, 2], True)
-        zd[0](k)
+        v['pd'][k] = mm6(q_stack(v['Qd'][k].T, RD), RD, B[k, 0], B[k, 1], B[k, 2], True)
+        A('d', k, 0)
+        A('d', k, 1)
 
     def part_g(k):
         lcopy(v['mga'].at[0], v['Mg'].at[k], 0, 7 + k).wait()
         lcopy(v['gga'].at[0], v['Gg'].at[k], 1, 7 + k).wait()
         lcopy(v['qga'].at[0], v['Qg'].at[k], 2, 7 + k).wait()
-        load_sum(v['Mg'], v['Gg'], v['Bg'], k, SQ)
+        load_sum(v['Mg'], v['Gg'], v['Bg'], k, SN)
         B = v['Bg']
-        v['pg'][k] = mm6(q_stack(v['Qg'][k], RE), RE, B[k, 0], B[k, 1], B[k, 2], True)
+        v['pg'][k] = mm6(q_stack(v['Qg'][k], RE), RE, B[k, 0], B[k, 1], B[k, 2])
         v['pgT'][k, RX:] = zero_rows
-        zg[0](k)
 
     def part_n(k):
         lcopy(v['mdn'].at[0], v['Mn'].at[k], 0, 4 + k).wait()
@@ -297,7 +328,8 @@
         return mm6(p3, rp, p3[:rp], p3[rp:2 * rp], p3[2 * rp:], True)
 
     def post_d(k):
-        zd[3](k)
+        W('d', k, 0)
+        W('d', k, 1)
         p3 = stack3(v['pdT'][k])
         B = v['Bd']
         v['yd'][k, :, :SQ] = mm6(p3, RD, B[k, 0], B[k, 1], B[k, 2])
@@ -305,10 +337,10 @@
         yd[0](k)
 
     def post_g(k):
-        zg[3](k)
+        W('g', k)
         p3 = stack3(v['pgT'][k])
         B = v['Bg']
-        v['yg'][k, :, :SN] = mm6(p3, RE, B[k, 0], B[k, 1], B[k, 2])
+        v['yg'][k, :, :SN] = mm6(p3, RE, B[k, 0], B[k, 1], B[k, 2], True)
         v['yg'][k, :, SN:384] = jnp.zeros((RE, 384 - SN), F32)
         v['yg'][k, :, 384:384 + RE] = gram(p3, RE)
         v['yg'][k, :, 384 + RE:] = jnp.zeros((RE, 128 - RE), F32)
@@ -323,94 +355,148 @@
         v['vn'][k, :, 384:384 + RE] = gram(p3, RE)
         v['vn'][k, :, 384 + RE:] = jnp.zeros((RE, 128 - RE), F32)
         v['vnT'][k, RX:] = zero_rows
-        zn[0](k)
-
-    def orth(l_ref, p_ref, y_ref, po, rt, k, r, rp, width):
+        A('G', k)
+
+    def orth_p(l_ref, p_ref, po, k, rp):
         l3 = stack3(l_ref[k, :, :rp])
         q3 = stack3(p_ref[k])
         po[k] = mm6(l3, rp, q3[:rp], q3[rp:2 * rp], q3[2 * rp:])
+
+    def orth_r(l_ref, y_ref, rt, k, rp, width, norm, lane):
+        l3 = stack3(l_ref[k, :, :rp])
         y3 = stack3(y_ref[k, :, :width])
         res = mm6(l3, rp, y3[:rp], y3[rp:2 * rp], y3[2 * rp:])
         rt[k] = res
-        return jnp.sum(res * res, axis=1, keepdims=True)
-
-    loop(ND, part_d)
-    loop(NE, part_n)
-
-    def ph3(k):
-        part_g(k)
-
-        @pl.when(k < ND)
-        def _():
-            zd[1](jnp.minimum(k, ND - 1))
-
-        @pl.when((k >= 1) & (k <= ND))
-        def _():
-            zd[2](jnp.clip(k - 1, 0, ND - 1))
-    loop(NG, ph3)
-    loop(NE, yn[1])
-    loop(NE, yn[2])
-    loop(NE, post_n)
-
-    def ph5(k):
-        zg[1](k)
-
-        @pl.when(k >= 1)
-        def _():
-            zg[2](jnp.maximum(k - 1, 0))
-
-        @pl.when(k < ND)
-        def _():
-            post_d(jnp.minimum(k, ND - 1))
-    loop(NG, ph5)
-    zg[2](NG - 1)
-    loop(NE, zn[1])
-    loop(NE, zn[2])
-    loop(ND, yd[1])
-    loop(ND, yd[2])
-    loop(NG, post_g)
+        col = jnp.sum(res * res, axis=1, keepdims=True)
+        here = lax.broadcasted_iota(jnp.int32, (rp, 128), 1) == lane
+        norm[:rp] = jnp.where(here, jnp.broadcast_to(col, (rp, 128)), norm[:rp])
+
+    def orth_d(k):
+        orth_p(v['Ld'], v['pdT'], v['po_d'], k, RD)
+        orth_r(v['Ld'], v['ydT'], v['rt_d'], k, RD, SQ, v['st'], k)
+
+    def orth_g(k):
+        orth_p(v['Lg'], v['pgT'], v['po_g'], k, RE)
+        orth_r(v['Lg'], v['ygT'], v['rt_g'], k, RE, SN, v['st'], ND + k)
 
     def take_d(k):
         yd[3](k)
         v['Ad'][k] = v['ydT'][k, :, SQ:]
-    loop(ND, take_d)
-    chol(v['Ad'], v['Ld'], range(ND), RD // 8, RD)
-    loop(NG, yg[1])
-    loop(NG, yg[2])
-
-    def take_n(k):
-        zn[3](k)
-        v['An'][k] = v['vnT'][k, :, 384:]
-        v['Ln'][k, RX:] = jnp.zeros((RE - RX, 128), F32)
-    loop(NE, take_n)
-    chol(v['An'], v['Ln'], range(NE), RX // 8, RE)
 
     def take_g(k):
         yg[3](k)
         v['Ag'][k] = v['ygT'][k, :, 384:]
         v['Lg'][k, RX:] = jnp.zeros((RE - RX, 128), F32)
-    loop(NG, take_g)
-    chol(v['Ag'], v['Lg'], range(NG), RX // 8, RE)
-
-    lane_sq = lax.broadcasted_iota(jnp.int32, (128, 128), 1)
+
+    def take_n(k):
+        W('G', k)
+        v['An'][k] = v['vnT'][k, :, 384:]
+        v['Ln'][k, RX:] = jnp.zeros((RE - RX, 128), F32)
+
+    def ST(n):
+        def go():
+            S(n)
+            T(n - 1)
+        return go
+
     v['st'][...] = jnp.zeros((128, 128), F32)
     v['ft'][...] = jnp.zeros((128, 128), F32)
 
-    def put(ref, col, rp, lane):
-        here = lax.broadcasted_iota(jnp.int32, (rp, 128), 1) == lane
-        ref[:rp] = jnp.where(here, jnp.broadcast_to(col, (rp, 128)), ref[:rp])
-
-    def orth_d(k):
-        put(v['st'], orth(v['Ld'], v['pdT'], v['ydT'], v['po_d'], v['rt_d'], k, RD, RD, SQ), RD, k)
-    loop(ND, orth_d)
-
-    def orth_n(k):
-        put(v['ft'], orth(v['Ln'], v['ynT'], v['vnT'], v['po_n'], v['rt_n'], k, RX, RE, SN), RE, k)
-    loop(NE, orth_n)
-
-    def orth_g(k):
-        put(v['st'], orth(v['Lg'], v['pgT'], v['ygT'], v['po_g'], v['rt_g'], k, RX, RE, SN), RE, ND + k)
-    loop(NG, orth_g)
+
+    for k in range(ND):
+        part_d(k)
+    part_n(0)
+    part_n(1)
+    S(0)
+    part_n(2)
+    part_g(0)
+    part_g(1)
+    ST(1)()
+    for k in range(NE):
+        yn[1](k)
+    part_g(2)
+    part_g(3)
+    ST(2)()
+    for k in range(NE):
+        yn[2](k)
+    ST(3)()
+    for k in range(NE):
+        post_n(k)
+    for k in range(4):
+        A('g', k)
+    ST(4)()
+    part_g(4)
+    part_g(5)
+    for k in range(4, NG):
+        A('g', k)
+    for k in range(NE):
+        A('Y', k)
+    ST(5)()
+    post_d(0)
+    ST(6)()
+    post_d(1)
+    yd[1](0)
+    ST(7)()
+    post_d(2)
+    yd[1](1)
+    yd[2](0)
+    for n in (8, 9, 10):
+        ST(n)()
+    T(10)
+    for k in range(NE):
+        take_n(k)
+    chol(v['An'], v['Ln'], [0, 1, 2], RX // 8, RE, [(2, lambda: S(11)), (9, ST(12))])
+    post_d(3)
+    yd[1](2)
+    yd[2](1)
+    for k in range(NE):
+        orth_p(v['Ln'], v['ynT'], v['po_n'], k, RE)
+    yd[1](3)
+    yd[2](2)
+    ST(13)()
+    post_g(0)
+    yd[2](3)
+    for k in range(ND):
+        take_d(k)
+    chol(v['Ad'], v['Ld'], [0, 1, 2, 3], RD // 8, RD, [(4, ST(14)), (11, ST(15))])
+    post_g(1)
+    yg[1](0)
+    ST(16)()
+    post_g(2)
+    yg[1](1)
+    yg[2](0)
+    orth_d(0)
+    yg[1](2)
+    yg[2](1)
+    ST(17)()
+    post_g(3)
+    yg[2](2)
+    for k in range(3):
+        take_g(k)
+    chol(v['Ag'], v['Lg'], [0, 1, 2], RX // 8, RE, [(3, ST(18)), (8, ST(19))])
+    post_g(4)
+    T(19)
+    yg[1](3)
+    post_g(5)
+    orth_d(1)
+    yg[1](4)
+    yg[2](3)
+    orth_d(2)
+    yg[1](5)
+    yg[2](4)
+    orth_d(3)
+    orth_g(0)
+    yg[2](5)
+    orth_g(1)
+    orth_g(2)
+    for k in range(3, NG):
+        take_g(k)
+    chol(v['Ag'], v['Lg'], [3, 4, 5], RX // 8, RE)
+    for k in range(NE):
+        W('Y', k)
+        orth_r(v['Ln'], v['vnT'], v['rt_n'], k, RE, SN, v['ft'], k)
+    for k in range(3, NG):
+        orth_g(k)
 
     v['sr'][0] = v['st'][...].T[:16]
     v['fr'][0] = v['ft'][...].T[:16]
@@ -432,9 +518,8 @@
 
     for c in copies:
         c.wait_send()
-    loop(ND, zd[4])
-    loop(NG, zg[4])
-    loop(NE, zn[4])
+    for piece in Z:
+        piece[4]()
     loop(ND, yd[4])
     loop(NG, yg[4])
     loop(NE, yn[4])
@@ -497,17 +582,17 @@
         rt = pad(v['rt_' + g][k])
         inv = v['inv_f'][:, k:k + 1] if g == 'n' else v['inv_t'][:, i:i + 1]
         qt = rt * jnp.broadcast_to(inv, rt.shape)
-        flip = g == 'n'
+        flip = g != 'd'
         for c in loads[i]:
             c.wait()
         m, gr, x = v['m' + g], v['g' + g], v['x' + g]
         eta = LEARN_RATE * (math.sqrt(2048 / 1408) if i >= 4 else 1.0)
         if flip:
-            q = qt.T
+            q = qt
             rhs = packs(pt)
             m[k] = m[k] + gr[k].astype(F32) - (1.0 - MOMENTUM) * prod(pack(rt.T), rhs)
             stores[i][0].start()
-            x[k] = x[k] - eta * prod(pack(q), rhs)
+            x[k] = x[k] - eta * prod(pack(qt.T), rhs)
             stores[i][1].start()
         else:
             lhs = pack(pt.T)
@@ -519,7 +604,7 @@
         if e is None:
             v['Q' + tag][...] = q
         else:
-            v['Q' + tag][e] = q[:, :RX]
+            v['Q' + tag][e] = q[:RX]
     for group in stores:
         for c in group:
             c.wait()
@@ -543,22 +628,25 @@
 
     def local_step(*blocks):
         mats = [blocks[4 * i:4 * i + 4] for i in range(7)]
+        for i in (4, 5):
+            mats[i] = tuple(jnp.swapaxes(a, 1, 2) for a in mats[i])
+        mats[6] = mats[6][:3] + (jnp.swapaxes(mats[6][3], 1, 2),)
         first = []
         for x, m, g, q in mats:
             first += [m, g, q]
         scratch = [
             vm(ND, SQ, SQ), vm(ND, SQ, SQ, dtype=BF16), vm(ND, SQ, RD),
-            vm(NG, SQ, SN), vm(NG, SQ, SN, dtype=BF16), vm(NG, SN, RX),
-            vm(NE, SN, SQ), vm(NE, SN, SQ, dtype=BF16), vm(NE, SN, RX),
-            vm(ND, 3, SQ, SQ, dtype=BF16), vm(NG, 3, SQ, SN, dtype=BF16), vm(NE, 3, SN, SQ, dtype=BF16)]
-        scratch += [vm(ND, RD, SQ)] * 4 + [vm(NG, RE, SQ)] * 4 + [vm(NE, RE, SQ)] * 4
+            vm(NG, SN, SQ), vm(NG, SN, SQ, dtype=BF16), vm(NG, RX, SN),
+            vm(NE, SN, SQ), vm(NE, SN, SQ, dtype=BF16), vm(NE, RX, SN),
+            vm(ND, 3, SQ, SQ, dtype=BF16), vm(NG, 3, SN, SQ, dtype=BF16), vm(NE, 3, SN, SQ, dtype=BF16)]
+        scratch += [vm(ND, RD, SQ)] * 3 + [vm(NG, RE, SQ)] * 3 + [vm(NE, RE, SQ)] * 3
         for n, rp, w in ((ND, RD, SQ + 128), (NG, RE, 512), (NE, RE, 512)):
-            scratch += [vm(n, rp, w), vm(n, rp // 2, w), vm(n, rp // 2, w), vm(n, rp // 2, w), vm(n, rp, w)]
+            scratch += [vm(n, rp, w), vm(n, rp // 2, w), vm(n, rp // 2, w), vm(n, rp, w)]
         for n, rp in ((ND, RD), (NG, RE), (NE, RE)):
             scratch += [vm(n, rp, 128), vm(n, rp, 128)]
         scratch += [vm(128, 128), vm(4, 16, 128), vm(128, 128), vm(4, 16, 128)]
         scratch += [dma((3, 13))]
-        scratch += [dma((3, n)) for n in (ND, ND, NG, NG, NE, NE)] * 2
+        scratch += [dma((3, n)) for n in (2 * ND, 2 * ND, NG, NG, 2 * NE, 2 * NE, ND, ND, NG, NG, NE, NE)]
         scratch += [dma((4,))] * 4
         shapes = [(ND, RD, SQ), (NG, RE, SQ), (NE, RE, SQ), (ND, RD, SQ), (NG, RE, SN), (NE, RE, SN), (128, 128), (128, 128)]
         mids = pl.pallas_call(
@@ -568,24 +656,26 @@
             out_specs=[vspec] * 8,
             scratch_shapes=scratch,
             name='comm',
-            compiler_params=pltpu.CompilerParams(collective_id=0, has_side_effects=True, vmem_limit_bytes=64 * 1024 * 1024 - 65536),
+            compiler_params=pltpu.CompilerParams(collective_id=0, has_side_effects=True, vmem_limit_bytes=VMEM_MAX),
         )(*first)
         second, shapes2, ospecs = [], [], []
         for x, m, g, q in mats:
             second += [x, m, g]
             shapes2 += [x, m, q]
             ospecs += [anyspec, anyspec, vspec]
-        res = pl.pallas_call(
+        res = list(pl.pallas_call(
             update_kernel,
             out_shape=[jax.ShapeDtypeStruct(a.shape, F32) for a in shapes2],
             in_specs=[vspec] * 8 + [anyspec] * 21,
             out_specs=ospecs,
             scratch_shapes=[vm(ND, SQ, SQ), vm(ND, SQ, SQ), vm(ND, SQ, SQ, dtype=BF16),
-                            vm(NG, SQ, SN), vm(NG, SQ, SN), vm(NG, SQ, SN, dtype=BF16),
+                            vm(NG, SN, SQ), vm(NG, SN, SQ), vm(NG, SN, SQ, dtype=BF16),
                             vm(NE, SN, SQ), vm(NE, SN, SQ), vm(NE, SN, SQ, dtype=BF16), dma((3, 13)), dma((2, 13))],
             name='update',
-            compiler_params=pltpu.CompilerParams(vmem_limit_bytes=64 * 1024 * 1024 - 65536),
-        )(*mids, *second)
+            compiler_params=pltpu.CompilerParams(vmem_limit_bytes=VMEM_MAX),
+        )(*mids, *second))
+        for i in (12, 13, 14, 15, 16, 17, 20):
+            res[i] = jnp.swapaxes(res[i], 1, 2)
         return tuple(res)
 
     return jax.shard_map(local_step, mesh=mesh, in_specs=in_specs, out_specs=out_specs, check_vma=False)

time: 248 us -> 139 us (0.56)
  Pallas kernels: 212 us -> 138 us
  local copies, waits for them, and re-layouts: 34.2 us -> 0 us
    pallas_call x1, Pallas kernels: 191 us -> 117 us  [local_step(): pl.pallas_call(comm_kernel, out_shape=[jax.ShapeDtypeStruct(s, F32) for s...]
    unnamed x23 -> x0, local copies, waits for them, and re-layouts: 19 us -> none
    pallas_call x7 -> x0, local copies, waits for them, and re-layouts: 15.1 us -> none  [local_step(): pl.pallas_call(update_kernel, out_shape=[jax.ShapeDtypeStruct(a.shape, F3...]
where the time goes in v2:
time: 139 us
  Pallas kernels  138 us (99%)
    pallas_call x1, Pallas kernels, local_step(): pl.pallas_call(comm_kernel, out_shape=[jax.ShapeDtypeStruct(s, F32) for s...  117 us
    pallas_call x1, Pallas kernels, local_step(): pl.pallas_call(update_kernel, out_shape=[jax.ShapeDtypeStruct(a.shape, F3...  21.3 us

profile of v2, /device:TPU:0, one launch (start us, length us, event | category | flops | bytes accessed | tf_op | source)
XLA Modules:
  0.0 138.9 jit_solution(7251125054115006188)
XLA Ops:
  0.7 116.8 %comm.1 = (f32[4,128,512]{2,1,0:T(8,128)}, f32[6,96,512]{2,1,0:T(8,128)}, f32[3,96,512]{2,1,0:T(8,128)}, f32[4,128,512]{2,1,0:T(8,128)}, f32[6,96,352]{2,1,0:T(8...) custom-call(f32[512,512]{1,0:T(8,128)} %refs_9_.3, bf16[512,512]{1,0:T(8,128)(2,1)} %refs_10_.3, ...), custom_call_target="tpu_custom_call" | custom-call | tf_op jit(solution)/shard_map/comm/pallas_call | solution.py:652
  117.5 21.3 %update.1 = (f32[512,512]{1,0:T(8,128)}, f32[512,512]{1,0:T(8,128)}, f32[512,128]{1,0:T(8,128)}, f32[512,512]{1,0:T(8,128)}, f32[512,512]{1,0:T(8,128)}, /*index...) custom-call(f32[4,128,512]{2,1,0:T(8,128)} %get-tuple-element.50.ref, ...), custom_call_target="tpu_custom_call" | custom-call | tf_op jit(solution)/shard_map/update/pallas_call | solution.py:666

commit v3 on v2

--- a/solution.py
+++ b/solution.py
@@ -9,12 +9,25 @@
 
 MOMENTUM = 0.9
 LEARN_RATE = 0.3
-VMEM_MAX = 58 * 1024 * 1024
+SLOTS = 4
+RING = 4
+COMM_VMEM = 26 * 1024 * 1024
+UPDATE_VMEM = 16 * 1024 * 1024
+TAGS = ('d0', 'd1', 'd2', 'd3', 'ga', 'up', 'dn')
 F32 = jnp.float32
 BF16 = jnp.bfloat16
 ND, NG, NE = 4, 6, 3
 RD, RE, RX = 128, 96, 88
 SQ, SN = 512, 352
+
+SCHEDULE = (
+    'Pd0 Pd1 Pn0 Pn1', 'Pn2 y2n0 Pd2 y2n1', 'y2n2 Pd3 S0 Pg0', 'Pg1 Pg2 S1 Pg3', 'y3n0 Pg4 Pg5 y3n1', 'S2 T0 Qn0 Qn1',
+    'y3n2 T1 S3 Qn2', 'T2 S4 Qd0 S5', 'T3 y2d0 T4 S6', 'S7 T5 Qd1 S8', 'S9 y2d1 S10 T6', 'y3d0 T7 Qd2 S11',
+    'T8 T9 y2d2 T10', 'y3d1 S12 Qd3 T11', 'y2d3 S13 y3d2 Cn012', '@4 T12 @6 S14', 'end y3d3 Qg0 T13', 'pn0 Cd0123 @0 S15',
+    'y2g0 @5 T14 @7', 'S16 @10 y3g0 @12', 'T15 S17 end Qg1', 'Qg2 S18 y2g1 T16', 'Qg3 y2g2 Od0 Od1', 'S19 y2g3 Qg4 T17',
+    'Od2 Od3 y2g4 y3g1', 'pn1 pn2 T18 Qg5', 'y3g2 y2g5 T19 Cg012', '@0 y3g3 @5 y3g4', 'end y3g5 Og0 Og1',
+    'Cg345 end Og2 Og3', 'Og4 Og5 rn0 rn1', 'rn2',
+)
 
 
 def split3(x):
@@ -41,16 +54,17 @@
     return jnp.concatenate(split3(x), axis=0)
 
 
-def load_sum(m_ref, g_ref, bs_ref, k, rows):
+def load_split(b_ref, sp_ref, k, rows, g_ref=None, j=0):
     step = 32
 
     def body(c, carry):
         sl = pl.ds(pl.multiple_of(c * step, step), step)
-        b = m_ref[k, sl, :] + g_ref[k, sl, :].astype(F32)
-        b1, b2, b3 = split3(b)
-        bs_ref[k, 0, sl, :] = b1
-        bs_ref[k, 1, sl, :] = b2
-        bs_ref[k, 2, sl, :] = b3
+        b = b_ref[k, sl, :]
+        if g_ref is not None:
+            b = b + g_ref[j, sl, :].astype(F32)
+            b_ref[k, sl, :] = b
+        for i, piece in enumerate(split3(b)):
+            sp_ref[i, sl, :] = piece
         return carry
 
     lax.fori_loop(0, rows // step, body, 0)
@@ -116,11 +130,12 @@
 
 
 def comm_kernel(*refs):
-    names = [
-        'md0', 'gd0', 'qd0', 'md1', 'gd1', 'qd1', 'md2', 'gd2', 'qd2', 'md3', 'gd3', 'qd3',
-        'mga', 'gga', 'qga', 'mup', 'gup', 'qup', 'mdn', 'gdn', 'qdn',
-        'po_d', 'po_g', 'po_n', 'rt_d', 'rt_g', 'rt_n', 'inv_t', 'inv_f',
-        'Md', 'Gd', 'Qd', 'Mg', 'Gg', 'Qg', 'Mn', 'Gn', 'Qn', 'Bd', 'Bg', 'Bn',
+    names = []
+    for t in TAGS:
+        names += ['x' + t, 'm' + t, 'g' + t, 'q' + t]
+    names += [
+        'po_d', 'po_g', 'po_n', 'rt_d', 'rt_g', 'rt_n', 'inv_t', 'inv_f', 'Bd', 'Bg', 'Bn', 'Xd', 'Xg', 'Xn',
+        'sp', 'Gd', 'Ge', 'Qd', 'Qg', 'Qn',
         'pd', 'pdT', 'pdB', 'pg', 'pgT', 'pgB', 'vn', 'vnT', 'vnB',
         'yd', 'yd1', 'yd2', 'ydT', 'yg', 'yg1', 'yg2', 'ygT', 'yn', 'yn1', 'yn2', 'ynT',
         'Ad', 'Ld', 'Ag', 'Lg', 'An', 'Ln', 'st', 'sr', 'ft', 'fr',
@@ -141,20 +156,44 @@
     def lcopy(src, dst, i, j):
         return pltpu.make_async_copy(src, dst, v['lsem'].at[i, j])
 
-    loads = []
-    for k in range(ND):
-        loads.append([lcopy(v[f'md{k}'], v['Md'].at[k], 0, k), lcopy(v[f'gd{k}'], v['Gd'].at[k], 1, k),
-                      lcopy(v[f'qd{k}'], v['Qd'].at[k], 2, k)])
-    for e in range(NE):
-        loads.append([lcopy(v['mdn'].at[e], v['Mn'].at[e], 0, ND + e), lcopy(v['gdn'].at[e], v['Gn'].at[e], 1, ND + e),
-                      lcopy(v['qdn'].at[e], v['Qn'].at[e], 2, ND + e)])
-    for k in range(NG):
-        m, g, q = ('mga', 'gga', 'qga') if k < 3 else ('mup', 'gup', 'qup')
-        loads.append([lcopy(v[m].at[k % 3], v['Mg'].at[k], 0, 7 + k), lcopy(v[g].at[k % 3], v['Gg'].at[k], 1, 7 + k),
-                      lcopy(v[q].at[k % 3], v['Qg'].at[k], 2, 7 + k)])
-    for group in loads:
-        for c in group:
-            c.start()
+    def source(c, g, k):
+        if g == 'd':
+            return v[c + TAGS[k]]
+        if g == 'n':
+            return v[c + 'dn'].at[k]
+        return v[c + ('ga' if k < 3 else 'up')].at[k % 3]
+
+    def load(c, g, k):
+        i = {'d': 0, 'n': ND, 'g': ND + NE}[g] + k
+        dst = v[('X' if c == 'x' else 'B') + g].at[k]
+        if c == 'g':
+            ref, j = place(g, k)
+            dst = v[ref].at[j]
+        if c == 'q':
+            dst = v['Q' + g].at[k]
+        return lcopy(source(c, g, k), dst, 'mgqx'.index(c), i)
+
+    def place(g, k):
+        if g == 'd':
+            return 'Gd', k % 2
+        return 'Ge', (k if g == 'n' else NE + k) % SLOTS
+
+    def refill(g, k):
+        if g == 'd':
+            nxt = ('d', k + 2)
+            ok = k + 2 < ND
+        else:
+            e = (k if g == 'n' else NE + k) + SLOTS
+            ok = e < NE + NG
+            nxt = ('g', e - NE)
+        if ok:
+            load('g', *nxt).start()
+
+    order = [('d', k) for k in range(ND)] + [('n', k) for k in range(NE)] + [('g', k) for k in range(NG)]
+    for g, k in order:
+        for c in 'mgq':
+            if c != 'g' or (k < 2 if g == 'd' else (g == 'n' or NE + k < SLOTS)):
+                load(c, g, k).start()
 
     barrier = pltpu.get_barrier_semaphore()
     for d in range(1, 4):
@@ -267,8 +306,7 @@
         Z.append(zpiece('vn', 'vnT', 'vnB', 'zs_n', 'zr_n', NE + k, k, 0, RX, 0, 384))
 
 
-    def A(*key):
-        Z[where[key]][0]()
+    keys = sorted(where, key=where.get)
 
     def S(n):
         Z[n][1]()
@@ -296,33 +334,25 @@
             qt = jnp.concatenate([qt, jnp.zeros((rp - qt.shape[0], qt.shape[1]), F32)], axis=0)
         return stack3(qt)
 
-    def part_d(k):
-        lcopy(v['md0'], v['Md'].at[k], 0, k).wait()
-        lcopy(v['gd0'], v['Gd'].at[k], 1, k).wait()
-        lcopy(v['qd0'], v['Qd'].at[k], 2, k).wait()
-        load_sum(v['Md'], v['Gd'], v['Bd'], k, SQ)
-        B = v['Bd']
-        v['pd'][k] = mm6(q_stack(v['Qd'][k].T, RD), RD, B[k, 0], B[k, 1], B[k, 2], True)
-        A('d', k, 0)
-        A('d', k, 1)
-
-    def part_g(k):
-        lcopy(v['mga'].at[0], v['Mg'].at[k], 0, 7 + k).wait()
-        lcopy(v['gga'].at[0], v['Gg'].at[k], 1, 7 + k).wait()
-        lcopy(v['qga'].at[0], v['Qg'].at[k], 2, 7 + k).wait()
-        load_sum(v['Mg'], v['Gg'], v['Bg'], k, SN)
-        B = v['Bg']
-        v['pg'][k] = mm6(q_stack(v['Qg'][k], RE), RE, B[k, 0], B[k, 1], B[k, 2])
-        v['pgT'][k, RX:] = zero_rows
-
-    def part_n(k):
-        lcopy(v['mdn'].at[0], v['Mn'].at[k], 0, 4 + k).wait()
-        lcopy(v['gdn'].at[0], v['Gn'].at[k], 1, 4 + k).wait()
-        lcopy(v['qdn'].at[0], v['Qn'].at[k], 2, 4 + k).wait()
-        load_sum(v['Mn'], v['Gn'], v['Bn'], k, SN)
-        B = v['Bn']
-        v['yn'][k] = mm6(q_stack(v['Qn'][k], RE), RE, B[k, 0], B[k, 1], B[k, 2])
-        yn[0](k)
+    def pieces(g):
+        rows = v['B' + g].shape[1]
+        return [v['sp'][i, :rows] for i in range(3)]
+
+    def part(g, k):
+        for c in 'mgq':
+            load(c, g, k).wait()
+        ref, j = place(g, k)
+        load_split(v['B' + g], v['sp'], k, v['B' + g].shape[1], v[ref], j)
+        refill(g, k)
+        load('x', g, k).start()
+        q = v['Q' + g][k]
+        own, trans = {'d': ('pd', True), 'g': ('pg', False), 'n': ('yn', False)}[g]
+        rp = RD if g == 'd' else RE
+        v[own][k] = mm6(q_stack(q.T if g == 'd' else q, rp), rp, *pieces(g), trans)
+        if g == 'g':
+            v['pgT'][k, RX:] = zero_rows
+        if g == 'n':
+            yn[0](k)
 
     def gram(p3, rp):
         return mm6(p3, rp, p3[:rp], p3[rp:2 * rp], p3[2 * rp:], True)
@@ -331,16 +361,16 @@
         W('d', k, 0)
         W('d', k, 1)
         p3 = stack3(v['pdT'][k])
-        B = v['Bd']
-        v['yd'][k, :, :SQ] = mm6(p3, RD, B[k, 0], B[k, 1], B[k, 2])
+        load_split(v['Bd'], v['sp'], k, v['Bd'].shape[1])
+        v['yd'][k, :, :SQ] = mm6(p3, RD, *pieces('d'))
         v['yd'][k, :, SQ:] = gram(p3, RD)
         yd[0](k)
 
     def post_g(k):
         W('g', k)
         p3 = stack3(v['pgT'][k])
-        B = v['Bg']
-        v['yg'][k, :, :SN] = mm6(p3, RE, B[k, 0], B[k, 1], B[k, 2], True)
+        load_split(v['Bg'], v['sp'], k, v['Bg'].shape[1])
+        v['yg'][k, :, :SN] = mm6(p3, RE, *pieces('g'), True)
         v['yg'][k, :, SN:384] = jnp.zeros((RE, 384 - SN), F32)
         v['yg'][k, :, 384:384 + RE] = gram(p3, RE)
         v['yg'][k, :, 384 + RE:] = jnp.zeros((RE, 128 - RE), F32)
@@ -349,13 +379,12 @@
     def post_n(k):
         yn[3](k)
         p3 = stack3(v['ynT'][k])
-        B = v['Bn']
-        v['vn'][k, :, :SN] = mm6(p3, RE, B[k, 0], B[k, 1], B[k, 2], True)
+        load_split(v['Bn'], v['sp'], k, v['Bn'].shape[1])
+        v['vn'][k, :, :SN] = mm6(p3, RE, *pieces('n'), True)
         v['vn'][k, :, SN:384] = jnp.zeros((RE, 384 - SN), F32)
         v['vn'][k, :, 384:384 + RE] = gram(p3, RE)
         v['vn'][k, :, 384 + RE:] = jnp.zeros((RE, 128 - RE), F32)
         v['vnT'][k, RX:] = zero_rows
-        A('G', k)
 
     def orth_p(l_ref, p_ref, po, k, rp):
         l3 = stack3(l_ref[k, :, :rp])
@@ -393,110 +422,60 @@
         v['An'][k] = v['vnT'][k, :, 384:]
         v['Ln'][k, RX:] = jnp.zeros((RE - RX, 128), F32)
 
-    def ST(n):
-        def go():
-            S(n)
-            T(n - 1)
-        return go
-
     v['st'][...] = jnp.zeros((128, 128), F32)
     v['ft'][...] = jnp.zeros((128, 128), F32)
 
 
-    for k in range(ND):
-        part_d(k)
-    part_n(0)
-    part_n(1)
-    S(0)
-    part_n(2)
-    part_g(0)
-    part_g(1)
-    ST(1)()
-    for k in range(NE):
-        yn[1](k)
-    part_g(2)
-    part_g(3)
-    ST(2)()
-    for k in range(NE):
-        yn[2](k)
-    ST(3)()
-    for k in range(NE):
-        post_n(k)
-    for k in range(4):
-        A('g', k)
-    ST(4)()
-    part_g(4)
-    part_g(5)
-    for k in range(4, NG):
-        A('g', k)
-    for k in range(NE):
-        A('Y', k)
-    ST(5)()
-    post_d(0)
-    ST(6)()
-    post_d(1)
-    yd[1](0)
-    ST(7)()
-    post_d(2)
-    yd[1](1)
-    yd[2](0)
-    for n in (8, 9, 10):
-        ST(n)()
-    T(10)
-    for k in range(NE):
-        take_n(k)
-    chol(v['An'], v['Ln'], [0, 1, 2], RX // 8, RE, [(2, lambda: S(11)), (9, ST(12))])
-    post_d(3)
-    yd[1](2)
-    yd[2](1)
-    for k in range(NE):
-        orth_p(v['Ln'], v['ynT'], v['po_n'], k, RE)
-    yd[1](3)
-    yd[2](2)
-    ST(13)()
-    post_g(0)
-    yd[2](3)
-    for k in range(ND):
-        take_d(k)
-    chol(v['Ad'], v['Ld'], [0, 1, 2, 3], RD // 8, RD, [(4, ST(14)), (11, ST(15))])
-    post_g(1)
-    yg[1](0)
-    ST(16)()
-    post_g(2)
-    yg[1](1)
-    yg[2](0)
-    orth_d(0)
-    yg[1](2)
-    yg[2](1)
-    ST(17)()
-    post_g(3)
-    yg[2](2)
-    for k in range(3):
-        take_g(k)
-    chol(v['Ag'], v['Lg'], [0, 1, 2], RX // 8, RE, [(3, ST(18)), (8, ST(19))])
-    post_g(4)
-    T(19)
-    yg[1](3)
-    post_g(5)
-    orth_d(1)
-    yg[1](4)
-    yg[2](3)
-    orth_d(2)
-    yg[1](5)
-    yg[2](4)
-    orth_d(3)
-    orth_g(0)
-    yg[2](5)
-    orth_g(1)
-    orth_g(2)
-    for k in range(3, NG):
-        take_g(k)
-    chol(v['Ag'], v['Lg'], [3, 4, 5], RX // 8, RE)
-    for k in range(NE):
+    made, sent = set(), [0]
+
+    def ship():
+        while sent[0] < len(Z) and keys[sent[0]][:2] in made:
+            Z[sent[0]][0]()
+            sent[0] += 1
+
+    def last_r(k):
         W('Y', k)
         orth_r(v['Ln'], v['vnT'], v['rt_n'], k, RE, SN, v['ft'], k)
-    for k in range(3, NG):
-        orth_g(k)
+
+    table = {'Pd': functools.partial(part, 'd'), 'Pn': functools.partial(part, 'n'), 'Pg': functools.partial(part, 'g'), 'Qd': post_d, 'Qn': post_n, 'Qg': post_g, 'Od': orth_d, 'Og': orth_g,
+             'pn': lambda k: orth_p(v['Ln'], v['ynT'], v['po_n'], k, RE), 'rn': last_r}
+    groups = {'d': ('Ad', 'Ld', RD, RD, take_d, yd), 'g': ('Ag', 'Lg', RX, RE, take_g, yg), 'n': ('An', 'Ln', RX, RE, take_n, yn)}
+
+    def do(word):
+        if word[0] == 'S':
+            S(int(word[1:]))
+        elif word[0] == 'T':
+            T(int(word[1:]))
+        elif word[0] == 'y':
+            groups[word[2]][5][int(word[1]) - 1](int(word[3]))
+        else:
+            k = int(word[2])
+            table[word[:2]](k)
+            if word[:2] in ('Pd', 'Pg'):
+                made.add((word[1], k))
+            if word[:2] == 'Qn':
+                made.update((('G', k), ('Y', k)))
+            ship()
+
+    words = [w for line in SCHEDULE for w in line.split()]
+    while words:
+        word = words.pop(0)
+        if word[0] != 'C':
+            do(word)
+            continue
+        a, l, r, rp, take, _ = groups[word[1]]
+        ks = [int(c) for c in word[2:]]
+        duties = []
+        while words[0] != 'end':
+            w = words.pop(0)
+            if w[0] == '@':
+                duties.append((int(w[1:]), []))
+            else:
+                duties[-1][1].append(w)
+        words.pop(0)
+        for k in ks:
+            take(k)
+        chol(v[a], v[l], ks, r // 8, rp, [(at, functools.partial(lambda todo: [do(w) for w in todo] and None, todo)) for at, todo in duties])
 
     v['sr'][0] = v['st'][...].T[:16]
     v['fr'][0] = v['ft'][...].T[:16]
@@ -520,24 +499,21 @@
         c.wait_send()
     for piece in Z:
         piece[4]()
+    for g, k in order:
+        load('x', g, k).wait()
     loop(ND, yd[4])
     loop(NG, yg[4])
     loop(NE, yn[4])
 
 
 def update_kernel(*refs):
-    names = ['po_d', 'po_g', 'po_n', 'rt_d', 'rt_g', 'rt_n', 'inv_t', 'inv_f']
-    ins = []
-    for g in ('d0', 'd1', 'd2', 'd3', 'ga', 'up', 'dn'):
-        ins += [f'x{g}', f'm{g}', f'g{g}']
-    outs = []
-    for g in ('d0', 'd1', 'd2', 'd3', 'ga', 'up', 'dn'):
-        outs += [f'X{g}', f'M{g}', f'Q{g}']
-    scr = ['xd', 'md', 'gd', 'xg', 'mg', 'gg', 'xn', 'mn', 'gn', 'lsem', 'osem']
-    v = dict(zip(names + ins + outs + scr, refs))
-    assert len(names + ins + outs + scr) == len(refs)
-    tags = [('d0', None), ('d1', None), ('d2', None), ('d3', None)] + [('ga', e) for e in range(3)] + \
-        [('up', e) for e in range(3)] + [('dn', e) for e in range(3)]
+    names = ['po_d', 'po_g', 'po_n', 'rt_d', 'rt_g', 'rt_n', 'inv_t', 'inv_f', 'Bd', 'Bg', 'Bn', 'Xd', 'Xg', 'Xn']
+    for t in TAGS:
+        names += ['X' + t, 'M' + t, 'Q' + t]
+    names += ['ms', 'xs', 'qd', 'qg', 'qn', 'osem']
+    v = dict(zip(names, refs))
+    assert len(names) == len(refs)
+    tags = [(t, None) for t in TAGS[:4]] + [(t, e) for t in TAGS[4:] for e in range(3)]
 
     def at(name, e):
         return v[name] if e is None else v[name].at[e]
@@ -549,16 +525,13 @@
             return 'g', i - 4
         return 'n', i - 10
 
-    loads, stores = [], []
+    stores = []
     for i, (tag, e) in enumerate(tags):
         g, k = slot(i)
-        loads.append([pltpu.make_async_copy(at(c + tag, e), v[c + g].at[k], v['lsem'].at[j, i])
-                      for j, c in enumerate(('m', 'g', 'x'))])
-        stores.append([pltpu.make_async_copy(v[c.lower() + g].at[k], at(c + tag, e), v['osem'].at[j, i])
-                       for j, c in enumerate(('M', 'X'))])
-    for group in loads:
-        for c in group:
-            c.start()
+        rows = v['B' + g].shape[1]
+        stores.append([pltpu.make_async_copy(v['ms'].at[i % RING, :rows], at('M' + tag, e), v['osem'].at[0, i]),
+                       pltpu.make_async_copy(v['xs'].at[i % RING, :rows], at('X' + tag, e), v['osem'].at[1, i]),
+                       pltpu.make_async_copy(v['q' + g].at[k], at('Q' + tag, e), v['osem'].at[2, i])])
 
     def pack(x):
         a, b, c = split3(x)
@@ -583,30 +556,26 @@
         inv = v['inv_f'][:, k:k + 1] if g == 'n' else v['inv_t'][:, i:i + 1]
         qt = rt * jnp.broadcast_to(inv, rt.shape)
         flip = g != 'd'
-        for c in loads[i]:
-            c.wait()
-        m, gr, x = v['m' + g], v['g' + g], v['x' + g]
-        eta = LEARN_RATE * (math.sqrt(2048 / 1408) if i >= 4 else 1.0)
+        q = qt[:RX] if flip else qt.T
+        v['q' + g][k] = q
+        stores[i][2].start()
+        eta = LEARN_RATE * (math.sqrt(2048 / 1408) if flip else 1.0)
         if flip:
-            q = qt
             rhs = packs(pt)
-            m[k] = m[k] + gr[k].astype(F32) - (1.0 - MOMENTUM) * prod(pack(rt.T), rhs)
-            stores[i][0].start()
-            x[k] = x[k] - eta * prod(pack(qt.T), rhs)
-            stores[i][1].start()
+            lhs_m, rhs_m, lhs_x, rhs_x = pack(rt.T), rhs, pack(qt.T), rhs
         else:
             lhs = pack(pt.T)
-            m[k] = m[k] + gr[k].astype(F32) - (1.0 - MOMENTUM) * prod(lhs, packs(rt))
-            stores[i][0].start()
-            x[k] = x[k] - eta * prod(lhs, packs(qt))
-            stores[i][1].start()
-            q = qt.T
-        if e is None:
-            v['Q' + tag][...] = q
-        else:
-            v['Q' + tag][e] = q[:RX]
-    for group in stores:
-        for c in group:
+            lhs_m, rhs_m, lhs_x, rhs_x = lhs, packs(rt), lhs, packs(qt)
+        rows = v['B' + g].shape[1]
+        if i >= RING:
+            stores[i - RING][0].wait()
+            stores[i - RING][1].wait()
+        v['ms'][i % RING, :rows] = v['B' + g][k] - (1.0 - MOMENTUM) * prod(lhs_m, rhs_m)
+        stores[i][0].start()
+        v['xs'][i % RING, :rows] = v['X' + g][k] - eta * prod(lhs_x, rhs_x)
+        stores[i][1].start()
+    for i, group in enumerate(stores):
+        for c in group[2:] if i < len(stores) - RING else group:
             c.wait()
 
 
@@ -623,7 +592,7 @@
     in_specs = (dense_w, dense_w, dense_w, dense_f) * 4 + (stack_w, stack_w, stack_w, stack_f) * 2 + (stack_w, stack_w, stack_w, down_f)
     out_specs = (dense_w, dense_w, dense_f) * 4 + (stack_w, stack_w, stack_f) * 2 + (stack_w, stack_w, down_f)
     dma = pltpu.SemaphoreType.DMA
-    anyspec = pl.BlockSpec(memory_space=pl.ANY)
+    hbm = pl.BlockSpec(memory_space=pltpu.HBM)
     vspec = pl.BlockSpec(memory_space=pltpu.VMEM)
 
     def local_step(*blocks):
@@ -631,49 +600,36 @@
         for i in (4, 5):
             mats[i] = tuple(jnp.swapaxes(a, 1, 2) for a in mats[i])
         mats[6] = mats[6][:3] + (jnp.swapaxes(mats[6][3], 1, 2),)
-        first = []
-        for x, m, g, q in mats:
-            first += [m, g, q]
-        scratch = [
-            vm(ND, SQ, SQ), vm(ND, SQ, SQ, dtype=BF16), vm(ND, SQ, RD),
-            vm(NG, SN, SQ), vm(NG, SN, SQ, dtype=BF16), vm(NG, RX, SN),
-            vm(NE, SN, SQ), vm(NE, SN, SQ, dtype=BF16), vm(NE, RX, SN),
-            vm(ND, 3, SQ, SQ, dtype=BF16), vm(NG, 3, SN, SQ, dtype=BF16), vm(NE, 3, SN, SQ, dtype=BF16)]
+        scratch = [vm(3, SQ, SQ, dtype=BF16), vm(2, SQ, SQ, dtype=BF16), vm(SLOTS, SN, SQ, dtype=BF16), vm(ND, SQ, RD), vm(NG, RX, SN), vm(NE, RX, SN)]
         scratch += [vm(ND, RD, SQ)] * 3 + [vm(NG, RE, SQ)] * 3 + [vm(NE, RE, SQ)] * 3
         for n, rp, w in ((ND, RD, SQ + 128), (NG, RE, 512), (NE, RE, 512)):
             scratch += [vm(n, rp, w), vm(n, rp // 2, w), vm(n, rp // 2, w), vm(n, rp, w)]
         for n, rp in ((ND, RD), (NG, RE), (NE, RE)):
             scratch += [vm(n, rp, 128), vm(n, rp, 128)]
         scratch += [vm(128, 128), vm(4, 16, 128), vm(128, 128), vm(4, 16, 128)]
-        scratch += [dma((3, 13))]
+        scratch += [dma((4, 13))]
         scratch += [dma((3, n)) for n in (2 * ND, 2 * ND, NG, NG, 2 * NE, 2 * NE, ND, ND, NG, NG, NE, NE)]
         scratch += [dma((4,))] * 4
-        shapes = [(ND, RD, SQ), (NG, RE, SQ), (NE, RE, SQ), (ND, RD, SQ), (NG, RE, SN), (NE, RE, SN), (128, 128), (128, 128)]
+        shapes = [(ND, RD, SQ), (NG, RE, SQ), (NE, RE, SQ), (ND, RD, SQ), (NG, RE, SN), (NE, RE, SN), (128, 128), (128, 128),
+                  (ND, SQ, SQ), (NG, SN, SQ), (NE, SN, SQ), (ND, SQ, SQ), (NG, SN, SQ), (NE, SN, SQ)]
         mids = pl.pallas_call(
             comm_kernel,
             out_shape=[jax.ShapeDtypeStruct(s, F32) for s in shapes],
-            in_specs=[anyspec] * 21,
-            out_specs=[vspec] * 8,
+            in_specs=[hbm] * 28,
+            out_specs=[vspec] * 14,
             scratch_shapes=scratch,
             name='comm',
-            compiler_params=pltpu.CompilerParams(collective_id=0, has_side_effects=True, vmem_limit_bytes=VMEM_MAX),
-        )(*first)
-        second, shapes2, ospecs = [], [], []
-        for x, m, g, q in mats:
-            second += [x, m, g]
-            shapes2 += [x, m, q]
-            ospecs += [anyspec, anyspec, vspec]
+            compiler_params=pltpu.CompilerParams(collective_id=0, has_side_effects=True, vmem_limit_bytes=COMM_VMEM),
+        )(*[pltpu.with_memory_space_constraint(a, pltpu.HBM) for m in mats for a in m])
         res = list(pl.pallas_call(
             update_kernel,
-            out_shape=[jax.ShapeDtypeStruct(a.shape, F32) for a in shapes2],
-            in_specs=[vspec] * 8 + [anyspec] * 21,
-            out_specs=ospecs,
-            scratch_shapes=[vm(ND, SQ, SQ), vm(ND, SQ, SQ), vm(ND, SQ, SQ, dtype=BF16),
-                            vm(NG, SN, SQ), vm(NG, SN, SQ), vm(NG, SN, SQ, dtype=BF16),
-                            vm(NE, SN, SQ), vm(NE, SN, SQ), vm(NE, SN, SQ, dtype=BF16), dma((3, 13)), dma((2, 13))],
+            out_shape=[jax.ShapeDtypeStruct(m[j].shape, F32) for m in mats for j in (0, 1, 3)],
+            in_specs=[vspec] * 14,
+            out_specs=[hbm] * 21,
+            scratch_shapes=[vm(RING, SQ, SQ), vm(RING, SQ, SQ), vm(ND, SQ, RD), vm(NG, RX, SN), vm(NE, RX, SN), dma((3, 13))],
             name='update',
-            compiler_params=pltpu.CompilerParams(vmem_limit_bytes=VMEM_MAX),
-        )(*mids, *second))
+            compiler_params=pltpu.CompilerParams(vmem_limit_bytes=UPDATE_VMEM),
+        )(*mids))
         for i in (12, 13, 14, 15, 16, 17, 20):
             res[i] = jnp.swapaxes(res[i], 1, 2)
         return tuple(res)

time: 139 us -> 104 us (0.75)
  Pallas kernels: 138 us -> 103 us
    pallas_call x1, Pallas kernels: 117 us -> 91.2 us  [local_step(): pl.pallas_call(comm_kernel, out_shape=[jax.ShapeDtypeStruct(s, F32) for s...]
    pallas_call x1, Pallas kernels: 21.3 us -> 11.3 us  [local_step(): pl.pallas_call(update_kernel, out_shape=[jax.ShapeDtypeStruct(m[j].shape,...]
where the time goes in v3:
time: 104 us; the launch traced here: 103 us
  Pallas kernels  103 us (99%)
    pallas_call x1, Pallas kernels, local_step(): pl.pallas_call(comm_kernel, out_shape=[jax.ShapeDtypeStruct(s, F32) for s...  91.2 us
    pallas_call x1, Pallas kernels, local_step(): pl.pallas_call(update_kernel, out_shape=[jax.ShapeDtypeStruct(m[j].shape,...  11.3 us

profile of v3, /device:TPU:0, one launch (start us, length us, event | category | flops | bytes accessed | tf_op | source)
XLA Modules:
  0.0 103.4 jit_solution(5894430807748502722)
XLA Ops:
  0.7 91.2 %comm.1 = (f32[4,128,512]{2,1,0:T(8,128)S(1)}, f32[6,96,512]{2,1,0:T(8,128)S(1)}, f32[3,96,512]{2,1,0:T(8,128)S(1)}, f32[4,128,512]{2,1,0:T(8,128)S(1)}, f32[6,9...) custom-call(f32[512,512]{1,0:T(8,128)} %refs_0_.1, ...), custom_call_target="tpu_custom_call" | custom-call | tf_op jit(solution)/shard_map/comm/pallas_call | solution.py:615
  91.9 11.3 %update.1 = (f32[512,512]{1,0:T(8,128)}, f32[512,512]{1,0:T(8,128)}, f32[512,128]{1,0:T(8,128)}, f32[512,512]{1,0:T(8,128)}, f32[512,512]{1,0:T(8,128)}, /*index...) custom-call(f32[4,128,512]{2,1,0:T(8,128)S(1)} %get-tuple-element.56, ...), custom_call_target="tpu_custom_call" | custom-call | tf_op jit(solution)/shard_map/update/pallas_call | solution.py:624

commit v4 on v3

--- a/solution.py
+++ b/solution.py
@@ -19,15 +19,13 @@
 ND, NG, NE = 4, 6, 3
 RD, RE, RX = 128, 96, 88
 SQ, SN = 512, 352
-
-SCHEDULE = (
-    'Pd0 Pd1 Pn0 Pn1', 'Pn2 y2n0 Pd2 y2n1', 'y2n2 Pd3 S0 Pg0', 'Pg1 Pg2 S1 Pg3', 'y3n0 Pg4 Pg5 y3n1', 'S2 T0 Qn0 Qn1',
-    'y3n2 T1 S3 Qn2', 'T2 S4 Qd0 S5', 'T3 y2d0 T4 S6', 'S7 T5 Qd1 S8', 'S9 y2d1 S10 T6', 'y3d0 T7 Qd2 S11',
-    'T8 T9 y2d2 T10', 'y3d1 S12 Qd3 T11', 'y2d3 S13 y3d2 Cn012', '@4 T12 @6 S14', 'end y3d3 Qg0 T13', 'pn0 Cd0123 @0 S15',
-    'y2g0 @5 T14 @7', 'S16 @10 y3g0 @12', 'T15 S17 end Qg1', 'Qg2 S18 y2g1 T16', 'Qg3 y2g2 Od0 Od1', 'S19 y2g3 Qg4 T17',
-    'Od2 Od3 y2g4 y3g1', 'pn1 pn2 T18 Qg5', 'y3g2 y2g5 T19 Cg012', '@0 y3g3 @5 y3g4', 'end y3g5 Og0 Og1',
-    'Cg345 end Og2 Og3', 'Og4 Og5 rn0 rn1', 'rn2',
-)
+DENSE_ITEMS = ((0, 0, 32), (0, 32, 32), (0, 64, 64)) + tuple((k, h, 64) for k in range(1, ND) for h in (0, 64))
+
+SCHEDULE = ''.join((
+    'iikkkkSkiSkjjSTjciTccSTShmSThmTShlmTSaTSlSSTaSeSTlSTTaTSeTSl',
+    'TSaCn3@ASTe@DT@ES@ISTEoSTeuuoSTbCd4@BTbS@ETS@HT@If@KS@LT@Mf@',
+    'OTESoobTSobqqqboTqsbfsvTCg3@Bf@GfErfrrvvCg3ErrrZssutttttt',
+))
 
 
 def split3(x):
@@ -136,10 +134,10 @@
     names += [
         'po_d', 'po_g', 'po_n', 'rt_d', 'rt_g', 'rt_n', 'inv_t', 'inv_f', 'Bd', 'Bg', 'Bn', 'Xd', 'Xg', 'Xn',
         'sp', 'Gd', 'Ge', 'Qd', 'Qg', 'Qn',
-        'pd', 'pdT', 'pdB', 'pg', 'pgT', 'pgB', 'vn', 'vnT', 'vnB',
-        'yd', 'yd1', 'yd2', 'ydT', 'yg', 'yg1', 'yg2', 'ygT', 'yn', 'yn1', 'yn2', 'ynT',
+        *[g + c for g in ('pd', 'pg', 'vn') for c in ('', 'T', 'B')],
+        *[c for g in 'dgn' for c in ('y' + g, g + '1', g + '2', 'y' + g + 'T')],
         'Ad', 'Ld', 'Ag', 'Lg', 'An', 'Ln', 'st', 'sr', 'ft', 'fr',
-        'lsem', 'zs_d', 'zr_d', 'zs_g', 'zr_g', 'zs_n', 'zr_n', 'ys_d', 'yr_d', 'ys_g', 'yr_g', 'ys_n', 'yr_n',
+        'lsem', *[a + g for a in 'zy' for g in ('s_d', 'r_d', 's_g', 'r_g', 's_n', 'r_n')],
         'ns', 'nr', 'fs', 'fr2']
     v = dict(zip(names, refs))
     assert len(names) == len(refs)
@@ -173,27 +171,29 @@
             dst = v['Q' + g].at[k]
         return lcopy(source(c, g, k), dst, 'mgqx'.index(c), i)
 
+    order = []
+    for c in SCHEDULE:
+        if c in 'ijk':
+            g = 'dng'['ijk'.index(c)]
+            order.append((g, sum(o[0] == g for o in order)))
+    dense = [o for o in order if o[0] == 'd']
+    experts = [o for o in order if o[0] != 'd']
+
     def place(g, k):
         if g == 'd':
             return 'Gd', k % 2
-        return 'Ge', (k if g == 'n' else NE + k) % SLOTS
+        return 'Ge', experts.index((g, k)) % SLOTS
 
     def refill(g, k):
-        if g == 'd':
-            nxt = ('d', k + 2)
-            ok = k + 2 < ND
-        else:
-            e = (k if g == 'n' else NE + k) + SLOTS
-            ok = e < NE + NG
-            nxt = ('g', e - NE)
-        if ok:
-            load('g', *nxt).start()
-
-    order = [('d', k) for k in range(ND)] + [('n', k) for k in range(NE)] + [('g', k) for k in range(NG)]
-    for g, k in order:
+        line, slots = (dense, 2) if g == 'd' else (experts, SLOTS)
+        rest = line[line.index((g, k)) + slots:]
+        if rest:
+            load('g', *rest[0]).start()
+
+    for o in order:
         for c in 'mgq':
-            if c != 'g' or (k < 2 if g == 'd' else (g == 'n' or NE + k < SLOTS)):
-                load(c, g, k).start()
+            if c != 'g' or o in dense[:2] or o in experts[:SLOTS]:
+                load(c, *o).start()
 
     barrier = pltpu.get_barrier_semaphore()
     for d in range(1, 4):
@@ -251,8 +251,8 @@
 
         return send, half, total, take, done
 
-    def yset(own, r1, r2, t, ss, rs, half):
-        own, r1, r2, t, ss, rs = v[own], v[r1], v[r2], v[t], v[ss], v[rs]
+    def yset(g, half):
+        own, r1, r2, t, ss, rs = [v[c] for c in ('y' + g, g + '1', g + '2', 'y' + g + 'T', 'ys_' + g, 'yr_' + g)]
         h = r1
         mine = pl.ds(pl.multiple_of(core * half, 8), half)
         theirs = pl.ds(pl.multiple_of((1 - core) * half, 8), half)
@@ -289,24 +289,21 @@
 
         return y1, y2, y3, y4, fin
 
-    Z = []
-    where = {}
-    for k in range(ND):
-        for h in range(2):
-            where['d', k, h] = len(Z)
-            Z.append(zpiece('pd', 'pdT', 'pdB', 'zs_d', 'zr_d', 2 * k + h, k, h * 64, 64, 0, SQ))
+    Z, keys = [], []
+
+    def line(kind, k, own, sems, i, row0, rows, col0, cols):
+        keys.append((kind, k))
+        Z.append(zpiece(own, own + 'T', own + 'B', 'zs_' + sems, 'zr_' + sems, i, k, row0, rows, col0, cols))
+
+    for i, (k, row0, rows) in enumerate(DENSE_ITEMS):
+        line('d', k, 'pd', 'd', i, row0, rows, 0, SQ)
     for k in range(NE):
-        where['G', k] = len(Z)
-        Z.append(zpiece('vn', 'vnT', 'vnB', 'zs_n', 'zr_n', k, k, 0, RX, 384, 128))
+        line('G', k, 'vn', 'n', k, 0, RX, 384, 128)
     for k in range(NG):
-        where['g', k] = len(Z)
-        Z.append(zpiece('pg', 'pgT', 'pgB', 'zs_g', 'zr_g', k, k, 0, RX, 0, SQ))
+        line('g', k, 'pg', 'g', 2 * k, 0, 48, 0, SQ)
+        line('g', k, 'pg', 'g', 2 * k + 1, 48, RX - 48, 0, SQ)
     for k in range(NE):
-        where['Y', k] = len(Z)
-        Z.append(zpiece('vn', 'vnT', 'vnB', 'zs_n', 'zr_n', NE + k, k, 0, RX, 0, 384))
-
-
-    keys = sorted(where, key=where.get)
+        line('Y', k, 'vn', 'n', NE + k, 0, RX, 0, 384)
 
     def S(n):
         Z[n][1]()
@@ -314,12 +311,14 @@
     def T(n):
         Z[n][2]()
 
-    def W(*key):
-        Z[where[key]][3]()
-
-    yd = yset('yd', 'yd1', 'yd2', 'ydT', 'ys_d', 'yr_d', RD // 2)
-    yg = yset('yg', 'yg1', 'yg2', 'ygT', 'ys_g', 'yr_g', RE // 2)
-    yn = yset('yn', 'yn1', 'yn2', 'ynT', 'ys_n', 'yr_n', RE // 2)
+    def W(kind, k):
+        for key, piece in zip(keys, Z):
+            if key == (kind, k):
+                piece[3]()
+
+    yd = yset('d', RD // 2)
+    yg = yset('g', RE // 2)
+    yn = yset('n', RE // 2)
 
     def loop(n, body):
         def go(k, carry):
@@ -358,8 +357,7 @@
         return mm6(p3, rp, p3[:rp], p3[rp:2 * rp], p3[2 * rp:], True)
 
     def post_d(k):
-        W('d', k, 0)
-        W('d', k, 1)
+        W('d', k)
         p3 = stack3(v['pdT'][k])
         load_split(v['Bd'], v['sp'], k, v['Bd'].shape[1])
         v['yd'][k, :, :SQ] = mm6(p3, RD, *pieces('d'))
@@ -400,14 +398,6 @@
         here = lax.broadcasted_iota(jnp.int32, (rp, 128), 1) == lane
         norm[:rp] = jnp.where(here, jnp.broadcast_to(col, (rp, 128)), norm[:rp])
 
-    def orth_d(k):
-        orth_p(v['Ld'], v['pdT'], v['po_d'], k, RD)
-        orth_r(v['Ld'], v['ydT'], v['rt_d'], k, RD, SQ, v['st'], k)
-
-    def orth_g(k):
-        orth_p(v['Lg'], v['pgT'], v['po_g'], k, RE)
-        orth_r(v['Lg'], v['ygT'], v['rt_g'], k, RE, SN, v['st'], ND + k)
-
     def take_d(k):
         yd[3](k)
         v['Ad'][k] = v['ydT'][k, :, SQ:]
@@ -426,10 +416,11 @@
     v['ft'][...] = jnp.zeros((128, 128), F32)
 
 
-    made, sent = set(), [0]
-
-    def ship():
-        while sent[0] < len(Z) and keys[sent[0]][:2] in made:
+    made, sent, copies, uses = set(), [0], [], {}
+
+    def ship(key=None):
+        made.add(key)
+        while sent[0] < len(Z) and keys[sent[0]] in made:
             Z[sent[0]][0]()
             sent[0] += 1
 
@@ -437,54 +428,64 @@
         W('Y', k)
         orth_r(v['Ln'], v['vnT'], v['rt_n'], k, RE, SN, v['ft'], k)
 
-    table = {'Pd': functools.partial(part, 'd'), 'Pn': functools.partial(part, 'n'), 'Pg': functools.partial(part, 'g'), 'Qd': post_d, 'Qn': post_n, 'Qg': post_g, 'Od': orth_d, 'Og': orth_g,
-             'pn': lambda k: orth_p(v['Ln'], v['ynT'], v['po_n'], k, RE), 'rn': last_r}
-    groups = {'d': ('Ad', 'Ld', RD, RD, take_d, yd), 'g': ('Ag', 'Lg', RX, RE, take_g, yg), 'n': ('An', 'Ln', RX, RE, take_n, yn)}
-
-    def do(word):
-        if word[0] == 'S':
-            S(int(word[1:]))
-        elif word[0] == 'T':
-            T(int(word[1:]))
-        elif word[0] == 'y':
-            groups[word[2]][5][int(word[1]) - 1](int(word[3]))
-        else:
-            k = int(word[2])
-            table[word[:2]](k)
-            if word[:2] in ('Pd', 'Pg'):
-                made.add((word[1], k))
-            if word[:2] == 'Qn':
-                made.update((('G', k), ('Y', k)))
-            ship()
-
-    words = [w for line in SCHEDULE for w in line.split()]
-    while words:
-        word = words.pop(0)
-        if word[0] != 'C':
-            do(word)
+    def send_norms(_):
+        v['sr'][0] = v['st'][...].T[:16]
+        v['fr'][0] = v['ft'][...].T[:16]
+        for d in range(1, 4):
+            copies.append(remote(v['sr'].at[0], v['sr'].at[d], v['ns'].at[d], v['nr'].at[d], {'tp': lax.rem(z + d, 4)}))
+            copies.append(remote(v['fr'].at[0], v['fr'].at[d], v['fs'].at[d], v['fr2'].at[d], {'fsdp': lax.rem(f + d, 4)}))
+        for c in copies:
+            c.start()
+
+    table = {'S': S, 'T': T, 'Z': send_norms, 'v': last_r, 'l': post_d, 'm': post_n, 'o': post_g,
+             'q': lambda k: orth_r(v['Ld'], v['ydT'], v['rt_d'], k, RD, SQ, v['st'], k),
+             'r': lambda k: orth_r(v['Lg'], v['ygT'], v['rt_g'], k, RE, SN, v['st'], ND + k),
+             's': lambda k: orth_p(v['Ld'], v['pdT'], v['po_d'], k, RD),
+             't': lambda k: orth_p(v['Lg'], v['pgT'], v['po_g'], k, RE),
+             'u': lambda k: orth_p(v['Ln'], v['ynT'], v['po_n'], k, RE)}
+    for letters, steps in (('ae', yd), ('bf', yg), ('ch', yn)):
+        table[letters[0]], table[letters[1]] = steps[1], steps[2]
+    for letter, g in zip('ijk', 'dng'):
+        table[letter] = functools.partial(part, g)
+    groups = {'d': ('Ad', 'Ld', RD, RD, take_d), 'g': ('Ag', 'Lg', RX, RE, take_g), 'n': ('An', 'Ln', RX, RE, take_n)}
+
+    def do(c):
+        k = uses.get(c, 0)
+        uses[c] = k + 1
+        table[c](k)
+        if c in 'ik':
+            ship(('d' if c == 'i' else 'g', k))
+        if c == 'm':
+            ship(('G', k))
+            ship(('Y', k))
+
+    def do_all(todo):
+        for c in todo:
+            do(c)
+
+    todo = list(SCHEDULE)
+    while todo:
+        c = todo.pop(0)
+        if c != 'C':
+            do(c)
             continue
-        a, l, r, rp, take, _ = groups[word[1]]
-        ks = [int(c) for c in word[2:]]
+        g, count = todo.pop(0), int(todo.pop(0))
+        a, l, r, rp, take = groups[g]
+        first = uses.get('C' + g, 0)
+        uses['C' + g] = first + count
         duties = []
-        while words[0] != 'end':
-            w = words.pop(0)
-            if w[0] == '@':
-                duties.append((int(w[1:]), []))
+        while todo[0] != 'E':
+            c = todo.pop(0)
+            if c == '@':
+                duties.append((ord(todo.pop(0)) - ord('A'), []))
             else:
-                duties[-1][1].append(w)
-        words.pop(0)
+                duties[-1][1].append(c)
+        todo.pop(0)
+        ks = list(range(first, first + count))
         for k in ks:
             take(k)
-        chol(v[a], v[l], ks, r // 8, rp, [(at, functools.partial(lambda todo: [do(w) for w in todo] and None, todo)) for at, todo in duties])
-
-    v['sr'][0] = v['st'][...].T[:16]
-    v['fr'][0] = v['ft'][...].T[:16]
-    copies = []
-    for d in range(1, 4):
-        copies.append(remote(v['sr'].at[0], v['sr'].at[d], v['ns'].at[d], v['nr'].at[d], {'tp': lax.rem(z + d, 4)}))
-        copies.append(remote(v['fr'].at[0], v['fr'].at[d], v['fs'].at[d], v['fr2'].at[d], {'fsdp': lax.rem(f + d, 4)}))
-    for c in copies:
-        c.start()
+        chol(v[a], v[l], ks, r // 8, rp, [(at, functools.partial(do_all, d)) for at, d in duties])
+
     for c in copies:
         c.wait_recv()
     pad = jnp.zeros((112, 128), F32)
@@ -608,7 +609,7 @@
             scratch += [vm(n, rp, 128), vm(n, rp, 128)]
         scratch += [vm(128, 128), vm(4, 16, 128), vm(128, 128), vm(4, 16, 128)]
         scratch += [dma((4, 13))]
-        scratch += [dma((3, n)) for n in (2 * ND, 2 * ND, NG, NG, 2 * NE, 2 * NE, ND, ND, NG, NG, NE, NE)]
+        scratch += [dma((3, n)) for n in (2 * ND + 1, 2 * ND + 1, 2 * NG, 2 * NG, 2 * NE, 2 * NE, ND, ND, NG, NG, NE, NE)]
         scratch += [dma((4,))] * 4
         shapes = [(ND, RD, SQ), (NG, RE, SQ), (NE, RE, SQ), (ND, RD, SQ), (NG, RE, SN), (NE, RE, SN), (128, 128), (128, 128),
                   (ND, SQ, SQ), (NG, SN, SQ), (NE, SN, SQ), (ND, SQ, SQ), (NG, SN, SQ), (NE, SN, SQ)]

time: 104 us -> 102 us (0.981)
  Pallas kernels: 103 us -> 101 us
    pallas_call x1, Pallas kernels: 91.2 us -> 89.7 us  [local_step(): pl.pallas_call(comm_kernel, out_shape=[jax.ShapeDtypeStruct(s, F32) for s...]
where the time goes in v4:
time: 102 us
  Pallas kernels  101 us (99%)
    pallas_call x1, Pallas kernels, local_step(): pl.pallas_call(comm_kernel, out_shape=[jax.ShapeDtypeStruct(s, F32) for s...  89.7 us
    pallas_call x1, Pallas kernels, local_step(): pl.pallas_call(update_kernel, out_shape=[jax.ShapeDtypeStruct(m[j].shape,...  11.3 us

profile of v4, /device:TPU:0, one launch (start us, length us, event | category | flops | bytes accessed | tf_op | source)
XLA Modules:
  0.0 101.8 jit_solution(10873593513010940230)
XLA Ops:
  0.7 89.7 %comm.1 = (f32[4,128,512]{2,1,0:T(8,128)S(1)}, f32[6,96,512]{2,1,0:T(8,128)S(1)}, f32[3,96,512]{2,1,0:T(8,128)S(1)}, f32[4,128,512]{2,1,0:T(8,128)S(1)}, f32[6,9...) custom-call(f32[512,512]{1,0:T(8,128)} %refs_0_.1, ...), custom_call_target="tpu_custom_call" | custom-call | tf_op jit(solution)/shard_map/comm/pallas_call | solution.py:616
  90.3 11.3 %update.1 = (f32[512,512]{1,0:T(8,128)}, f32[512,512]{1,0:T(8,128)}, f32[512,128]{1,0:T(8,128)}, f32[512,512]{1,0:T(8,128)}, f32[512,512]{1,0:T(8,128)}, /*index...) custom-call(f32[4,128,512]{2,1,0:T(8,128)S(1)} %get-tuple-element.56, ...), custom_call_target="tpu_custom_call" | custom-call | tf_op jit(solution)/shard_map/update/pallas_call | solution.py:625
